TPU v7x, 32 devices: a whole 2x2x4 slice. The times are simulated.
32 devices in a mesh: gx: 4 (over x, core), gy: 4 (over z), gz: 2 (over y).
Axes of the slice: x: 2, y: 2, z: 4, core: 2. Of those that a mesh axis runs over, the one named last changes fastest.
Arguments:
- velocity: float32 [3, 32, 128, 512], P(None, 'gz', 'gy', 'gx'), may hold values from -14 to 14, as said below
- geometry: bfloat16 [6, 32, 128, 512], P(None, 'gz', 'gy', 'gx'), may hold values from -0.015 to 0.041, as said below
- mass_weights: bfloat16 [32, 128, 512], P('gz', 'gy', 'gx'), may hold values from 0.0099487305 to 0.099609375
Outputs:
- residual: float32 [3, 32, 128, 512], P(None, 'gz', 'gy', 'gx')
- kinetic: float32 [], replicated
- enstrophy: float32 [], replicated
Inputs may be any that keep to these rules, and one draw needn't show every extreme that they name: `velocity`: coincident points of neighbouring elements hold equal values, and points on the outer boundary of the grid hold zero. `geometry`: at every point the matrix [[g0, g3, g4], [g3, g1, g5], [g4, g5, g2]] is positive definite.
All inputs are finite; a program needn't handle non-finite values.
Results may differ from a plain program's by a relative error of at most 0.0003.
Values sent between devices are 32-bit elements; how exact they have to be, the bound alone decides.
A program may use at most 128 MiB of HBM per device.

v0:
```python
import jax
import jax.numpy as jnp
import numpy as np
from jax import lax
from jax.sharding import PartitionSpec as P

ORDER = 7


def padded_2(block, sides, width):
    for axis, dim in sides:
        count = lax.axis_size(axis)
        forward = [(i, i + 1) for i in range(count - 1)]
        backward = [(target, source) for source, target in forward]
        low = lax.ppermute(
            lax.slice_in_dim(block, block.shape[dim] - width, None, axis=dim), axis, forward
        )
        high = lax.ppermute(lax.slice_in_dim(block, 0, width, axis=dim), axis, backward)
        block = jnp.concatenate([low, block, high], axis=dim)
    return block


def gll_derivative(poly_order):
    node_count = poly_order + 1
    abscissa = np.cos(np.pi * np.arange(node_count) / poly_order)
    legendre = np.zeros((node_count, node_count))
    for newton_step in range(60):
        legendre[:, 0] = 1.0
        legendre[:, 1] = abscissa
        for degree in range(2, node_count):
            legendre[:, degree] = (
                (2 * degree - 1) * abscissa * legendre[:, degree - 1]
                - (degree - 1) * legendre[:, degree - 2]
            ) / degree
        abscissa = abscissa - (abscissa * legendre[:, poly_order] - legendre[:, poly_order - 1]) / (
            node_count * legendre[:, poly_order]
        )
    abscissa = abscissa[::-1]
    end_values = legendre[::-1, poly_order]
    spacing = abscissa[:, None] - abscissa[None, :] + np.eye(node_count)
    deriv_table = end_values[:, None] / end_values[None, :] / spacing
    deriv_table = deriv_table * (1.0 - np.eye(node_count))
    deriv_table[0, 0] = -poly_order * node_count / 4.0
    deriv_table[poly_order, poly_order] = poly_order * node_count / 4.0
    return deriv_table.astype(np.float32)


def derive(source, matrix, which_dim):
    highest = lax.Precision.HIGHEST
    points = matrix.shape[0]
    extent = source.shape
    block_table = jnp.kron(jnp.eye(extent[which_dim] // points, dtype=jnp.float32), matrix)
    if which_dim == 3:
        return jnp.einsum("czyx,wx->czyw", source, block_table, precision=highest)
    if which_dim == 2:
        return jnp.einsum("czyx,wy->czwx", source, block_table, precision=highest)
    return jnp.einsum("czyx,wz->cwyx", source, block_table, precision=highest)


def metric(geometry, slot_id):
    return geometry[slot_id].astype(jnp.float32)[None]


def apply_local(velocity, geometry, matrix):
    grad_r = derive(velocity, matrix, 3)
    grad_s = derive(velocity, matrix, 2)
    grad_t = derive(velocity, matrix, 1)
    flux_r = (
        metric(geometry, 0) * grad_r + metric(geometry, 3) * grad_s + metric(geometry, 4) * grad_t
    )
    flux_s = (
        metric(geometry, 3) * grad_r + metric(geometry, 1) * grad_s + metric(geometry, 5) * grad_t
    )
    flux_t = (
        metric(geometry, 4) * grad_r + metric(geometry, 5) * grad_s + metric(geometry, 2) * grad_t
    )
    enstrophy_part = jnp.sum(grad_r * flux_r + grad_s * flux_s + grad_t * flux_t)
    transposed = matrix.T
    applied = derive(flux_r, transposed, 3) + derive(flux_s, transposed, 2)
    applied = applied + derive(flux_t, transposed, 1)
    return (applied, enstrophy_part)


def assemble_padded(padded, which_dim, inner):
    center = lax.slice_in_dim(padded, 1, inner + 1, axis=which_dim)
    next_val = lax.slice_in_dim(padded, 2, inner + 2, axis=which_dim)
    prev_val = lax.slice_in_dim(padded, 0, inner, axis=which_dim)
    position = lax.broadcasted_iota(jnp.int32, center.shape, which_dim)
    points = ORDER + 1
    result = center + jnp.where(position % points == points - 1, next_val, 0.0)
    return result + jnp.where(position % points == 0, prev_val, 0.0)


def per_device(velocity, geometry, mass_weights):
    matrix = jnp.asarray(gll_derivative(ORDER), jnp.float32)
    planes, rows, columns = (velocity.shape[1], velocity.shape[2], velocity.shape[3])
    mass_float = mass_weights.astype(jnp.float32)
    kinetic_part = 0.5 * jnp.sum(mass_float[None] * velocity * velocity)
    applied, enstrophy_part = apply_local(velocity, geometry, matrix)
    kinetic, enstrophy = lax.psum((kinetic_part, enstrophy_part), ("gx", "gy", "gz"))
    stacked = jnp.concatenate([applied, mass_float[None]], 0)
    padded = padded_2(stacked, (("gx", 3),), 1)
    summed = assemble_padded(padded, 3, columns)
    padded = padded_2(summed, (("gy", 2),), 1)
    summed = assemble_padded(padded, 2, rows)
    padded = padded_2(summed, (("gz", 1),), 1)
    summed = assemble_padded(padded, 1, planes)
    extent = (planes, rows, columns)
    column_at = lax.broadcasted_iota(jnp.int32, extent, 2)
    row_at = lax.broadcasted_iota(jnp.int32, extent, 1)
    plane_at = lax.broadcasted_iota(jnp.int32, extent, 0)
    edge_cols = (lax.axis_index("gx") == 0) & (column_at == 0) | (
        lax.axis_index("gx") == lax.axis_size("gx") - 1
    ) & (column_at == columns - 1)
    edge_rows = (lax.axis_index("gy") == 0) & (row_at == 0) | (
        lax.axis_index("gy") == lax.axis_size("gy") - 1
    ) & (row_at == rows - 1)
    edge_planes = (lax.axis_index("gz") == 0) & (plane_at == 0) | (
        lax.axis_index("gz") == lax.axis_size("gz") - 1
    ) & (plane_at == planes - 1)
    interior = jnp.logical_not(edge_cols | edge_rows | edge_planes)
    rayleigh = enstrophy / (2.0 * kinetic)
    residual = jnp.where(interior[None], summed[:3] - rayleigh * summed[3][None] * velocity, 0.0)
    return (residual, kinetic, enstrophy)


def solution(mesh):
    in_specs = (P(None, "gz", "gy", "gx"), P(None, "gz", "gy", "gx"), P("gz", "gy", "gx"))
    out_specs = (P(None, "gz", "gy", "gx"), P(), P())
    return jax.shard_map(
        per_device, mesh=mesh, in_specs=in_specs, out_specs=out_specs, check_vma=False
    )
```

profile of v0, /device:TPU:0, one launch (start us, length us, event | category | flops | bytes accessed | tf_op | source)
XLA Modules:
  0.0 90.5 jit_solution(7652265839731211381)
XLA Ops:
  0.6 0.0 copy-start.8
  0.6 0.0 copy-start.9
  0.7 0.6 copy-done.8
  1.3 0.0 copy-done.9
  1.3 0.1 broadcast_multiply_fusion.4
  1.4 0.1 reshape.77
  1.5 0.1 reshape.74
  1.6 0.1 broadcast_multiply_fusion.2
  1.7 0.1 reshape.76
  1.8 0.1 reshape.73
  1.9 1.8 %fusion.47 = (f32[16,32,128]{2,1,0:T(8,128)}, f32[1,16,32,128]{3,2,1,0:T(8,128)}) fusion(bf16[16,32,128]{2,1,0:T(8,128)(2,1)} %param.6), kind=kLoop, calls=%fused_computation.104 | loop fusion | flops 65536 | bytes 655360 | tf_op jit(solution)/shard_map/convert_element_type | solution.py:97
  3.6 1.1 %bitcast_convert_fusion.5 = (f32[16,32,128]{2,1,0:T(8,128)S(1)}, f32[16,32,128]{2,1,0:T(8,128)}, f32[16,32,128]{2,1,0:T(8,128)}, f32[16,32,128]{2,1,0:T(8,128)S(...) fusion(bf16[6,16,32,128]{3,2,1,0:T(8,128)(2,1)S(1)} %copy-done.7), kind=kLoop, calls=%fused_computation.73 | loop fusion | flops 393216 | bytes 2359296 | tf_op jit(solution)/shard_map/mul | solution.py:69
  4.7 0.2 broadcast_multiply_fusion
  4.9 0.5 reshape.75
  5.4 0.5 reshape.72
  5.9 0.6 copy-done
  6.5 1.1 %fusion.24 = f32[16,3,32,128]{3,0,2,1:T(8,128)S(1)} fusion(f32[3,16,32,128]{3,2,1,0:T(8,128)S(1)} %copy-done, f32[16,16,1,1]{1,0,2,3:T(8,128)S(1)} %reshape.74), kind=kOutput, calls=%fused_computation.53 | convolution fusion | flops 37748736 | bytes 1573888 | tf_op jit(solution)/shard_map/czyx,wz->cwyx/dot_general | solution.py:57
  7.7 0.8 convolution_bitcast_fusion.2
  8.5 0.1 copy-done.1
  8.7 0.1 copy-done.3
  8.7 0.1 copy-done.4
  8.8 0.1 copy-done.5
  8.9 2.2 %fusion.21 = (f32[]{:T(128)}, f32[3,16,32,128]{3,2,1,0:T(8,128)S(1)}, f32[3,16,32,128]{3,2,1,0:T(8,128)S(1)}) fusion(f32[3,16,32,128]{3,2,1,0:T(8,128)S(1)} %convolution_bitcast_fusion.2, f32[16,3,32,128]{3,0,2,1:T(8,128)S(1)} %fusion.24, f32[16,32,128]{2,1,0:T(8,128)S(1)} %copy-done.4, f32[16,32,128]{2,1,0:T(8,128)S(1)} %copy-done.3, ...), kind=kOutput, calls=%fused_computation.50 | convolution fusion | flops 79626240 | bytes 5509124 | tf_op jit(solution)/shard_map/czyx,wy->czwx/dot_general | solution.py:56
  11.1 1.1 %fusion.22 = f32[16,3,32,128]{3,0,2,1:T(8,128)S(1)} fusion(f32[3,16,32,128]{3,2,1,0:T(8,128)S(1)} %get-tuple-element.6, f32[16,16,1,1]{1,0,2,3:T(8,128)S(1)} %reshape.77), kind=kOutput, calls=%fused_computation.51 | convolution fusion | flops 37748736 | bytes 1573888 | tf_op jit(solution)/shard_map/czyx,wz->cwyx/dot_general | solution.py:57
  12.3 1.3 %convolution_bitcast_fusion = f32[3,16,32,128]{3,2,1,0:T(8,128)S(1)} fusion(f32[3,16,32,128]{3,2,1,0:T(8,128)S(1)} %get-tuple-element.27, f32[3,16,32,128]{3,2,1,0:T(8,128)S(1)} %convolution_bitcast_fusion.2, f32[16,3,32,128]{3,0,2,1:T(8,128)S(1)} %fusion.24, f32[16,32,128]{2,1,0:T(8,128)S(1)} %copy-done.4, f32[16,32,128]{2,1,0:T(8,128)S(1)} %copy-done.3, ...), kind=kOutput, calls=%fused_computation.10 | convolution fusion | flops 76480512 | bytes 3936256 | tf_op jit(solution)/shard_map/czyx,wy->czwx/dot_general | solution.py:56
  13.6 1.4 %fusion = f32[3,16,32,128]{3,2,1,0:T(8,128)S(1)} fusion(f32[3,16,32,128]{3,2,1,0:T(8,128)S(1)} %convolution_bitcast_fusion, f32[16,3,32,128]{3,0,2,1:T(8,128)S(1)} %fusion.22, f32[3,16,32,128]{3,2,1,0:T(8,128)S(1)} %get-tuple-element.27, f32[3,16,32,128]{3,2,1,0:T(8,128)S(1)} %convolution_bitcast_fusion.2, f32[16,3,32,128]{3,0,2,1:T(8,128)S(1)} %fusion.24, ...), kind=kOutput, calls=%fused_computation.13 | convolution fusion | flops 303366144 | bytes 5570560 | tf_op jit(solution)/shard_map/czyx,wx->czyw/dot_general | solution.py:54
  14.9 1.4 %fusion.1 = (f32[4,16,32,1]{3,2,1,0:T(8,128)S(1)}, f32[4,16,32,1]{3,2,1,0:T(8,128)}) fusion(f32[3,16,32,128]{3,2,1,0:T(8,128)S(1)} %fusion, f32[1,16,32,128]{3,2,1,0:T(8,128)S(1)} %copy-done.2), kind=kLoop, calls=%fused_computation.17 | loop fusion | flops 4096 | bytes 1064960 | tf_op jit(solution)/shard_map/concatenate | solution.py:101
  16.3 1.7 %copy.21 = f32[4,16,32,1]{2,1,3,0:T(8,128)S(1)} copy(f32[4,16,32,1]{3,2,1,0:T(8,128)} %get-tuple-element.12) | data formatting | bytes 16384 | tf_op jit(solution)/shard_map/slice | solution.py:16
  18.0 2.4 %collective-permute-start.1 = (f32[4,16,32,1]{2,1,3,0:T(8,128)S(1)}, f32[4,16,32,1]{2,1,3,0:T(8,128)S(1)}, u32[]{:S(2)}, u32[]{:S(2)}) collective-permute-start(f32[4,16,32,1]{2,1,3,0:T(8,128)S(1)} %copy.21), channel_id=1, source_target_pairs={{0,8},{8,16},{16,24},{1,9},{9,17},{17,25},{2,10},{10,18},{18,26},{... | collective-permute-start | bytes 24584 | tf_op jit(solution)/shard_map/ppermute | solution.py:15
  20.4 0.0 copy-start.6
  20.4 0.4 copy.19
  20.9 1.3 %collective-permute-start = (f32[4,16,32,1]{2,1,3,0:T(8,128)S(1)}, f32[4,16,32,1]{2,1,3,0:T(8,128)S(1)}, u32[]{:S(2)}, u32[]{:S(2)}) collective-permute-start(f32[4,16,32,1]{2,1,3,0:T(8,128)S(1)} %copy.19), channel_id=1, source_target_pairs={{8,0},{16,8},{24,16},{9,1},{17,9},{25,17},{10,2},{18,10},{26,18},{... | collective-permute-start | bytes 24584 | tf_op jit(solution)/shard_map/ppermute | solution.py:18
  22.2 0.8 fusion.15
  23.1 0.1 or_not_fusion
  23.2 2.9 %collective-permute-done = f32[4,16,32,1]{2,1,3,0:T(8,128)S(1)} collective-permute-done((f32[4,16,32,1]{2,1,3,0:T(8,128)S(1)}, f32[4,16,32,1]{2,1,3,0:T(8,128)S(1)}, u32[]{:S(2)}, u32[]{:S(2)}) %collective-permute-start) | collective-permute-done | bytes 8224 | tf_op jit(solution)/shard_map/ppermute | solution.py:18
  26.0 1.4 %copy.20 = f32[4,16,32,1]{3,2,1,0:T(8,128)} copy(f32[4,16,32,1]{2,1,3,0:T(8,128)S(1)} %collective-permute-done) | data formatting | bytes 16384 | tf_op jit(solution)/shard_map/ppermute | solution.py:18
  27.5 1.4 %copy.22 = f32[4,16,32,1]{3,2,1,0:T(8,128)} copy(f32[4,16,32,1]{2,1,3,0:T(8,128)S(1)} %collective-permute-done.1) | data formatting | bytes 16384 | tf_op jit(solution)/shard_map/ppermute | solution.py:15
  28.9 2.4 %fusion.4 = f32[4,16,32,128]{3,2,1,0:T(8,128)S(1)} fusion(f32[1,16,32,128]{3,2,1,0:T(8,128)S(1)} %copy-done.2, f32[3,16,32,128]{3,2,1,0:T(8,128)S(1)} %fusion, f32[4,16,32,1]{3,2,1,0:T(8,128)} %copy.22, f32[4,16,32,1]{3,2,1,0:T(8,128)} %copy.20, s32[128]{0:T(128)S(1)} %get-tuple-element.28, s32[128]{0:T(128)S(1)} %get-tuple-element.29, ...), kind=kLoop, calls=%fused_computation.20 | loop fusion | flops 3145728 | bytes 2114688 | tf_op jit(solution)/shard_map/add | solution.py:91
  31.4 1.3 %collective-permute-start.2 = (f32[4,16,1,128]{3,2,1,0:T(1,128)S(1)}, f32[4,16,1,128]{3,2,1,0:T(1,128)S(1)}, u32[]{:S(2)}, u32[]{:S(2)}) collective-permute-start(f32[4,16,1,128]{3,2,1,0:T(1,128)S(1)} %get-tuple-element.9), channel_id=1, source_target_pairs={{2,0},{4,2},{6,4},{3,1},{5,3},{7,5},{10,8},{12,10},{14,12},{11,9},... | collective-permute-start | bytes 98312 | tf_op jit(solution)/shard_map/ppermute | solution.py:18
  32.7 4.5 %collective-permute-start.3 = (f32[4,16,1,128]{3,2,1,0:T(1,128)S(1)}, f32[4,16,1,128]{3,2,1,0:T(1,128)S(1)}, u32[]{:S(2)}, u32[]{:S(2)}) collective-permute-start(f32[4,16,1,128]{3,2,1,0:T(1,128)S(1)} %get-tuple-element.10), channel_id=1, source_target_pairs={{0,2},{2,4},{4,6},{1,3},{3,5},{5,7},{8,10},{10,12},{12,14},{9,11},... | collective-permute-start | bytes 98312 | tf_op jit(solution)/shard_map/ppermute | solution.py:15
  37.9 41.7 %all-reduce = (f32[]{:T(128)}, f32[]{:T(128)}) all-reduce(f32[]{:T(128)} %get-tuple-element.5, f32[]{:T(128)S(6)} %mul_shard_map.6), channel_id=1, replica_groups=mesh['gx'=4,'gy'=4,'gz'=2] {'gx','gy','gz'}, use_global_device_ids=true, to_apply=%region_1.2 | all-reduce | flops 2 | bytes 16 | tf_op jit(solution)/shard_map/psum | solution.py:100
  81.0 0.4 fusion.10
  81.4 1.3 %collective-permute-start.4 = (f32[4,1,32,128]{3,2,1,0:T(8,128)S(1)}, f32[4,1,32,128]{3,2,1,0:T(8,128)S(1)}, u32[]{:S(2)}, u32[]{:S(2)}) collective-permute-start(f32[4,1,32,128]{3,2,1,0:T(8,128)S(1)} %get-tuple-element.7), channel_id=1, source_target_pairs={{1,0},{3,2},{5,4},{7,6},{9,8},{11,10},{13,12},{15,14},{17,16},{19,... | collective-permute-start | bytes 196616 | tf_op jit(solution)/shard_map/ppermute | solution.py:18
  82.7 4.5 %collective-permute-start.5 = (f32[4,1,32,128]{3,2,1,0:T(8,128)S(1)}, f32[4,1,32,128]{3,2,1,0:T(8,128)S(1)}, u32[]{:S(2)}, u32[]{:S(2)}) collective-permute-start(f32[4,1,32,128]{3,2,1,0:T(8,128)S(1)} %get-tuple-element.8), channel_id=1, source_target_pairs={{0,1},{2,3},{4,5},{6,7},{8,9},{10,11},{12,13},{14,15},{16,17},{18,... | collective-permute-start | bytes 196616 | tf_op jit(solution)/shard_map/ppermute | solution.py:15
  87.2 0.3 collective-permute-done.4
  87.5 1.6 %collective-permute-done.5 = f32[4,1,32,128]{3,2,1,0:T(8,128)S(1)} collective-permute-done((f32[4,1,32,128]{3,2,1,0:T(8,128)S(1)}, f32[4,1,32,128]{3,2,1,0:T(8,128)S(1)}, u32[]{:S(2)}, u32[]{:S(2)}) %collective-permute-start.5) | collective-permute-done | bytes 65568 | tf_op jit(solution)/shard_map/ppermute | solution.py:15
  89.1 0.2 fusion.6
  89.4 1.1 %fusion.16 = f32[3,16,32,128]{3,2,1,0:T(8,128)} fusion(f32[4,16,32,128]{3,2,1,0:T(8,128)S(1)} %fusion.6, f32[3,16,32,128]{3,2,1,0:T(8,128)S(1)} %copy-done, f32[16,32,128]{2,1,0:T(8,128)S(1)} %fusion.36, pred[16,32,128]{2,1,0:T(8,128)(4,1)S(1)} %or_not_fusion), kind=kLoop, calls=%fused_computation.41 | loop fusion | flops 589824 | bytes 2686976 | tf_op jit(solution)/shard_map/jit(_where)/select_n | solution.py:123
  (28 shorter events, 0.2 us)
Async XLA Ops:
  0.6 0.7 copy-start.8
  0.6 0.7 copy-start.9
  0.7 3.0 %copy-start.7 = (bf16[6,16,32,128]{3,2,1,0:T(8,128)(2,1)S(1)}, bf16[6,16,32,128]{3,2,1,0:T(8,128)(2,1)}, u32[]{:S(2)}) copy-start(bf16[6,16,32,128]{3,2,1,0:T(8,128)(2,1)} %param.5) | copy-start | bytes 2359300
  5.4 1.1 %copy-start = (f32[3,16,32,128]{3,2,1,0:T(8,128)S(1)}, f32[3,16,32,128]{3,2,1,0:T(8,128)}, u32[]{:S(2)}) copy-start(f32[3,16,32,128]{3,2,1,0:T(8,128)} %param.4) | copy-start | bytes 2359300
  7.7 1.0 %copy-start.1 = (f32[16,32,128]{2,1,0:T(8,128)S(1)}, f32[16,32,128]{2,1,0:T(8,128)}, u32[]{:S(2)}) copy-start(f32[16,32,128]{2,1,0:T(8,128)} %get-tuple-element.15) | copy-start | bytes 786436
  7.7 1.0 %copy-start.3 = (f32[16,32,128]{2,1,0:T(8,128)S(1)}, f32[16,32,128]{2,1,0:T(8,128)}, u32[]{:S(2)}) copy-start(f32[16,32,128]{2,1,0:T(8,128)} %get-tuple-element.14) | copy-start | bytes 786436
  7.7 1.1 %copy-start.4 = (f32[16,32,128]{2,1,0:T(8,128)S(1)}, f32[16,32,128]{2,1,0:T(8,128)}, u32[]{:S(2)}) copy-start(f32[16,32,128]{2,1,0:T(8,128)} %get-tuple-element.18) | copy-start | bytes 786436
  7.7 1.2 %copy-start.5 = (f32[16,32,128]{2,1,0:T(8,128)S(1)}, f32[16,32,128]{2,1,0:T(8,128)}, u32[]{:S(2)}) copy-start(f32[16,32,128]{2,1,0:T(8,128)} %get-tuple-element.17) | copy-start | bytes 786436
  13.6 1.4 %copy-start.2 = (f32[1,16,32,128]{3,2,1,0:T(8,128)S(1)}, f32[1,16,32,128]{3,2,1,0:T(8,128)}, u32[]{:S(2)}) copy-start(f32[1,16,32,128]{3,2,1,0:T(8,128)} %get-tuple-element.20) | copy-start | bytes 786436
  18.0 9.5 %collective-permute-start.1 = (f32[4,16,32,1]{2,1,3,0:T(8,128)S(1)}, f32[4,16,32,1]{2,1,3,0:T(8,128)S(1)}, u32[]{:S(2)}, u32[]{:S(2)}) collective-permute-start(f32[4,16,32,1]{2,1,3,0:T(8,128)S(1)} %copy.21), channel_id=1, source_target_pairs={{0,8},{8,16},{16,24},{1,9},{9,17},{17,25},{2,10},{10,18},{18,26},{... | collective-permute-start | bytes 24584 | tf_op jit(solution)/shard_map/ppermute | solution.py:15
  20.4 1.8 %copy-start.6 = (f32[16,32,128]{2,1,0:T(8,128)S(1)}, f32[16,32,128]{2,1,0:T(8,128)}, u32[]{:S(2)}) copy-start(f32[16,32,128]{2,1,0:T(8,128)} %get-tuple-element.19) | copy-start | bytes 786436
  20.9 5.2 %collective-permute-start = (f32[4,16,32,1]{2,1,3,0:T(8,128)S(1)}, f32[4,16,32,1]{2,1,3,0:T(8,128)S(1)}, u32[]{:S(2)}, u32[]{:S(2)}) collective-permute-start(f32[4,16,32,1]{2,1,3,0:T(8,128)S(1)} %copy.19), channel_id=1, source_target_pairs={{8,0},{16,8},{24,16},{9,1},{17,9},{25,17},{10,2},{18,10},{26,18},{... | collective-permute-start | bytes 24584 | tf_op jit(solution)/shard_map/ppermute | solution.py:18
  31.4 49.6 %collective-permute-start.2 = (f32[4,16,1,128]{3,2,1,0:T(1,128)S(1)}, f32[4,16,1,128]{3,2,1,0:T(1,128)S(1)}, u32[]{:S(2)}, u32[]{:S(2)}) collective-permute-start(f32[4,16,1,128]{3,2,1,0:T(1,128)S(1)} %get-tuple-element.9), channel_id=1, source_target_pairs={{2,0},{4,2},{6,4},{3,1},{5,3},{7,5},{10,8},{12,10},{14,12},{11,9},... | collective-permute-start | bytes 98312 | tf_op jit(solution)/shard_map/ppermute | solution.py:18
  32.7 48.3 %collective-permute-start.3 = (f32[4,16,1,128]{3,2,1,0:T(1,128)S(1)}, f32[4,16,1,128]{3,2,1,0:T(1,128)S(1)}, u32[]{:S(2)}, u32[]{:S(2)}) collective-permute-start(f32[4,16,1,128]{3,2,1,0:T(1,128)S(1)} %get-tuple-element.10), channel_id=1, source_target_pairs={{0,2},{2,4},{4,6},{1,3},{3,5},{5,7},{8,10},{10,12},{12,14},{9,11},... | collective-permute-start | bytes 98312 | tf_op jit(solution)/shard_map/ppermute | solution.py:15
  81.4 6.2 %collective-permute-start.4 = (f32[4,1,32,128]{3,2,1,0:T(8,128)S(1)}, f32[4,1,32,128]{3,2,1,0:T(8,128)S(1)}, u32[]{:S(2)}, u32[]{:S(2)}) collective-permute-start(f32[4,1,32,128]{3,2,1,0:T(8,128)S(1)} %get-tuple-element.7), channel_id=1, source_target_pairs={{1,0},{3,2},{5,4},{7,6},{9,8},{11,10},{13,12},{15,14},{17,16},{19,... | collective-permute-start | bytes 196616 | tf_op jit(solution)/shard_map/ppermute | solution.py:18
  82.7 6.4 %collective-permute-start.5 = (f32[4,1,32,128]{3,2,1,0:T(8,128)S(1)}, f32[4,1,32,128]{3,2,1,0:T(8,128)S(1)}, u32[]{:S(2)}, u32[]{:S(2)}) collective-permute-start(f32[4,1,32,128]{3,2,1,0:T(8,128)S(1)} %get-tuple-element.8), channel_id=1, source_target_pairs={{0,1},{2,3},{4,5},{6,7},{8,9},{10,11},{12,13},{14,15},{16,17},{18,... | collective-permute-start | bytes 196616 | tf_op jit(solution)/shard_map/ppermute | solution.py:15
where the time goes:
time: 91.1 us; the launch traced here: 90.5 us
  blocking collectives  41.7 us (46%)
  starting transfers between devices  15.4 us (17%)
  other arithmetic  9.7 us (11%)
  local copies, waits for them, and re-layouts  8.03 us (9%)
  matrix products  7.95 us (9%)
  waiting for transfers between devices  4.74 us (5%)
  between operations  2.95 us (3%)
    psum x1, blocking collectives, per_device(): lax.psum((kinetic_part, enstrophy_part), ('gx', 'gy', 'gz'))  41.7 us
    ppermute x3, starting transfers between devices, padded_2(): lax.ppermute(lax.slice_in_dim(block, block.shape[dim] - width, None, axis...  11.5 us
    ppermute x3, starting transfers between devices, padded_2(): lax.ppermute(lax.slice_in_dim(block, 0, width, axis=dim), axis, backward)  3.88 us
    dot_general x2, matrix products, derive(): return jnp.einsum('czyx,wy->czwx', source, block_table, precision=highest)  3.5 us
    ppermute x3, waiting for transfers between devices, padded_2(): lax.ppermute(lax.slice_in_dim(block, 0, width, axis=dim), axis, backward)  3.16 us
    add x3, other arithmetic, assemble_padded(): return result + jnp.where(position % points == 0, prev_val, 0.0)  3.01 us
    dot_general x2, matrix products, derive(): return jnp.einsum('czyx,wz->cwyx', source, block_table, precision=highest)  2.29 us
    dot_general x2, matrix products, derive(): return jnp.einsum('czyx,wx->czyw', source, block_table, precision=highest)  2.15 us
  transfers between devices with their start and end apart: 6, of which 3 were waited for; matrix products, arithmetic and copies ran while one was open for 3% of the time, Pallas kernels for 0%

commit v1 on v0

v1 whole, which is shorter than its diff:
```python
import functools
import itertools

import jax
import jax.numpy as jnp
import numpy as np
from jax import lax
from jax.experimental import pallas as pl
from jax.experimental.pallas import tpu as pltpu
from jax.sharding import PartitionSpec as P

ORDER = 7
PTS = ORDER + 1
MESH = pl.DeviceIdType.MESH
AXES = ("gx", "gy", "gz")
XOFF = [o for o in itertools.product((-1, 0, 1), repeat=3) if o[0] != 0]
YZOFF = [o for o in itertools.product((-1, 0, 1), repeat=3) if o[0] == 0 and o[1] != 0 and o[2] != 0]
YOFF = [(0, -1, 0), (0, 1, 0)]
ZOFF = [(0, 0, -1), (0, 0, 1)]
OFFS = sorted(XOFF + YZOFF + YOFF + ZOFF, key=lambda o: -sum(map(abs, o)))


def gll_derivative(poly_order):
    node_count = poly_order + 1
    abscissa = np.cos(np.pi * np.arange(node_count) / poly_order)
    legendre = np.zeros((node_count, node_count))
    for newton_step in range(60):
        legendre[:, 0] = 1.0
        legendre[:, 1] = abscissa
        for degree in range(2, node_count):
            legendre[:, degree] = (
                (2 * degree - 1) * abscissa * legendre[:, degree - 1]
                - (degree - 1) * legendre[:, degree - 2]
            ) / degree
        abscissa = abscissa - (abscissa * legendre[:, poly_order] - legendre[:, poly_order - 1]) / (
            node_count * legendre[:, poly_order]
        )
    abscissa = abscissa[::-1]
    end_values = legendre[::-1, poly_order]
    spacing = abscissa[:, None] - abscissa[None, :] + np.eye(node_count)
    deriv_table = end_values[:, None] / end_values[None, :] / spacing
    deriv_table = deriv_table * (1.0 - np.eye(node_count))
    deriv_table[0, 0] = -poly_order * node_count / 4.0
    deriv_table[poly_order, poly_order] = poly_order * node_count / 4.0
    return deriv_table.astype(np.float32)


def split_np(m):
    hi = m.astype(jnp.bfloat16)
    lo = (m - hi.astype(np.float32)).astype(jnp.bfloat16)
    return hi, lo


def tables(rows, cols):
    d = gll_derivative(ORDER)
    out = []
    for mat in (d, d.T):
        hi, lo = split_np(np.kron(np.eye(cols // PTS, dtype=np.float32), mat.T))
        zero = np.zeros_like(lo)
        out.append(np.block([[hi, lo], [hi, zero]]))
        hi, lo = split_np(np.kron(np.eye(PTS * rows // PTS, dtype=np.float32), mat))
        out.append(np.stack([hi, lo]))
    pick = np.zeros((2 * cols, 2 * cols), np.float32)
    for base in (0, cols):
        pick[base, :cols] = 1.0
        pick[base + cols - 1, cols:] = 1.0
    out.append(pick.astype(jnp.bfloat16))
    put = np.zeros((2 * cols, cols), np.float32)
    put[:cols, cols - 1] = 1.0
    put[cols:, 0] = 1.0
    out.append(put.astype(jnp.bfloat16))
    return [jnp.asarray(t) for t in out]


def split(x):
    hi = x.astype(jnp.bfloat16)
    lo = (x - hi.astype(jnp.float32)).astype(jnp.bfloat16)
    return hi, lo


def dot(a, b):
    return jnp.dot(a, b, preferred_element_type=jnp.float32)


def along_x(pair, table):
    cols = table.shape[1] // 2
    r = dot(jnp.concatenate(pair, axis=1), table)
    return r[:, :cols] + r[:, cols:]


def along_y(pair, hi, lo):
    cols = pair[0].shape[1]
    r = dot(hi, jnp.concatenate(pair, axis=1))
    return r[:, :cols] + r[:, cols:] + dot(lo, pair[0])


def along_z(planes, mat):
    out = []
    for w in range(PTS):
        acc = planes[0] * float(mat[w, 0])
        for z in range(1, PTS):
            acc = acc + planes[z] * float(mat[w, z])
        out.append(acc)
    return out


def kernel(
    sizes,
    v_hbm, g_hbm, m_hbm, dx_ref, dy_ref, tx_ref, ty_ref, pick_ref, put_ref,
    a_out, m_out, s_out,
    v, g, m, flux, field, pack, yface, yzrow, rpack, ryface, rzface, ryz, part, parts,
    in_sem, send_sem, recv_sem, ssend, srecv,
):
    nx, ny, nz = sizes
    count = nx * ny * nz
    planes, rows, cols = v.shape[1:]
    layers = planes // PTS
    yel = rows // PTS
    half = cols // 2
    ix, iy, iz = (lax.axis_index(a) for a in AXES)
    me = (ix * ny + iy) * nz + iz
    d = gll_derivative(ORDER)

    loads = [
        pltpu.make_async_copy(src, dst, in_sem.at[k])
        for k, (src, dst) in enumerate(((m_hbm, m), (v_hbm, v), (g_hbm, g)))
    ]
    for c in loads:
        c.start()

    def peer_id(step):
        p = lax.rem(me + step, count)
        return {"gx": p // (ny * nz), "gy": lax.rem(p // nz, ny), "gz": lax.rem(p, nz)}

    barrier = pltpu.get_barrier_semaphore()

    @pl.loop(1, count)
    def _(step):
        pl.semaphore_signal(barrier, inc=1, device_id=peer_id(step), device_id_type=MESH)

    four = (PTS, yel, PTS, cols)
    ye_at = lax.broadcasted_iota(jnp.int32, four, 1)
    k_at = lax.broadcasted_iota(jnp.int32, four, 2)
    z_at = lax.broadcasted_iota(jnp.int32, four, 0)
    lane = lax.broadcasted_iota(jnp.int32, four, 3)
    lane2 = lax.broadcasted_iota(jnp.int32, (PTS * rows, cols), 1)
    row2 = lax.broadcasted_iota(jnp.int32, (PTS * rows, cols), 0)

    def assemble_xy(x):
        n = PTS * rows
        x = (
            x
            + jnp.where((lane2 % PTS == ORDER) & (lane2 < cols - 1), pltpu.roll(x, cols - 1, 1), 0.0)
            + jnp.where((lane2 % PTS == 0) & (lane2 > 0), pltpu.roll(x, 1, 1), 0.0)
        )
        return (
            x
            + jnp.where((row2 % PTS == ORDER) & (row2 % rows < rows - 1), pltpu.roll(x, n - 1, 0), 0.0)
            + jnp.where((row2 % PTS == 0) & (row2 % rows > 0), pltpu.roll(x, 1, 0), 0.0)
        )

    def finish_channel(c):
        for e in range(1, layers):
            low = field[c, e * PTS - 1]
            high = field[c, e * PTS]
            both = low + high
            field[c, e * PTS - 1] = both
            field[c, e * PTS] = both
        lo_acc = jnp.zeros((PTS, cols), jnp.float32)
        hi_acc = jnp.zeros((PTS, cols), jnp.float32)
        base = (c % 2) * half
        for e in range(layers):
            x = field[c, pl.ds(e * PTS, PTS)].reshape(PTS * rows, cols)
            r = dot(jnp.concatenate(split(x), axis=1), pick_ref[...])
            hit = lane == base + (e * PTS + z_at) * yel + ye_at
            lo_acc = lo_acc + jnp.sum(jnp.where(hit, r[:, :cols].reshape(four), 0.0), axis=(0, 1))
            hi_acc = hi_acc + jnp.sum(jnp.where(hit, r[:, cols:].reshape(four), 0.0), axis=(0, 1))
        pair = c // 2
        pack[0, pair] = pack[0, pair] + lo_acc
        pack[1, pair] = pack[1, pair] + hi_acc
        for side, y in ((0, 0), (1, rows - 1)):
            face = field[c, :, y, :]
            yface[side, c] = face
            yzrow[side, 0, c] = face[0:1]
            yzrow[side, 1, c] = face[planes - 1:planes]

    pack[...] = jnp.zeros(pack.shape, jnp.float32)
    loads[0].wait()
    for e in range(layers):
        x = m[pl.ds(e * PTS, PTS)].astype(jnp.float32).reshape(PTS * rows, cols)
        field[3, pl.ds(e * PTS, PTS)] = assemble_xy(x).reshape(PTS, rows, cols)
    finish_channel(3)
    loads[1].wait()
    loads[2].wait()

    def gradients(step, acc):
        kin, ens = acc
        c = step // layers
        at = pl.ds(pl.multiple_of((step % layers) * PTS, PTS), PTS)
        block = v[c, at]
        flat = block.reshape(PTS * rows, cols)
        mass = m[at].astype(jnp.float32)
        kin = kin + jnp.sum((mass * block * block).reshape(-1, PTS, cols), axis=0)
        pair = split(flat)
        gr = along_x(pair, dx_ref[...]).reshape(block.shape)
        gs = along_y(pair, dy_ref[0], dy_ref[1]).reshape(block.shape)
        gt = jnp.stack(along_z([block[z] for z in range(PTS)], d))
        g0, g1, g2, g3, g4, g5 = (g[k, at].astype(jnp.float32) for k in range(6))
        fr = g0 * gr + g3 * gs + g4 * gt
        fs = g3 * gr + g1 * gs + g5 * gt
        ft = g4 * gr + g5 * gs + g2 * gt
        ens = ens + jnp.sum((gr * fr + gs * fs + gt * ft).reshape(-1, PTS, cols), axis=0)
        flux[0, c, at] = fr
        flux[1, c, at] = fs
        flux[2, c, at] = ft
        return kin, ens

    zero = jnp.zeros((PTS, cols), jnp.float32)
    kin, ens = lax.fori_loop(0, 3 * layers, gradients, (zero, zero))
    mine = jnp.concatenate(
        [jnp.sum(kin, 0, keepdims=True) * 0.5, jnp.sum(ens, 0, keepdims=True)], axis=0
    )
    part[...] = mine
    parts[me] = mine

    pl.semaphore_wait(barrier, count - 1)

    def scalar_copy(step):
        return pltpu.make_async_remote_copy(
            src_ref=part, dst_ref=parts.at[me], send_sem=ssend, recv_sem=srecv,
            device_id=peer_id(step), device_id_type=MESH,
        )

    @pl.loop(1, count)
    def _(step):
        scalar_copy(step).start()

    @pl.loop(0, 3)
    def _(c):
        for e in range(layers):
            at = pl.ds(e * PTS, PTS)
            fr = flux[0, c, at].reshape(PTS * rows, cols)
            fs = flux[1, c, at].reshape(PTS * rows, cols)
            ft = flux[2, c, at]
            x = along_x(split(fr), tx_ref[...]) + along_y(split(fs), ty_ref[0], ty_ref[1])
            z = jnp.stack(along_z([ft[k] for k in range(PTS)], d.T))
            field[c, at] = assemble_xy(x + z.reshape(x.shape)).reshape(PTS, rows, cols)
        finish_channel(c)

    here = (ix, iy, iz)

    def there(off):
        ok = None
        for o, i, n in zip(off, here, sizes):
            if o:
                t = (i > 0) if o < 0 else (i < n - 1)
                ok = t if ok is None else ok & t
        return ok

    def side(o):
        return (o + 1) // 2

    def copy_to(off):
        n = OFFS.index(off)
        opp = tuple(-o for o in off)
        slot = OFFS.index(opp)
        if off[0]:
            src, dst = pack.at[side(off[0])], rpack.at[XOFF.index(opp)]
        elif off[1] and off[2]:
            src, dst = yzrow.at[side(off[1]), side(off[2])], ryz.at[YZOFF.index(opp)]
        elif off[1]:
            src, dst = yface.at[side(off[1])], ryface.at[YOFF.index(opp)]
        else:
            plane = 0 if off[2] < 0 else planes - 1
            src, dst = field.at[:, plane], rzface.at[ZOFF.index(opp)]
        return pltpu.make_async_remote_copy(
            src_ref=src, dst_ref=dst, send_sem=send_sem.at[n], recv_sem=recv_sem.at[slot],
            device_id={a: i + o for a, i, o in zip(AXES, here, off)}, device_id_type=MESH,
        )

    for off in OFFS:
        @pl.when(there(off))
        def _(off=off):
            copy_to(off).start()

    for off in OFFS:
        @pl.when(there(off))
        def _(off=off):
            n = OFFS.index(off)
            if off[0]:
                dst = rpack.at[XOFF.index(off)]
            elif off[1] and off[2]:
                dst = ryz.at[YZOFF.index(off)]
            elif off[1]:
                dst = ryface.at[YOFF.index(off)]
            else:
                dst = rzface.at[ZOFF.index(off)]
            pltpu.make_async_copy(dst, dst, recv_sem.at[n]).wait()

    pshape = (PTS, cols)
    plane_lane = lax.broadcasted_iota(jnp.int32, pshape, 1)
    prow = lax.broadcasted_iota(jnp.int32, pshape, 0)
    pz = (plane_lane % half) // yel
    pye = plane_lane % yel
    halo = [[None, None], [None, None]]
    for s, dx in ((0, -1), (1, 1)):
        for pair in range(2):
            acc = jnp.zeros(pshape, jnp.float32)
            for off in XOFF:
                if off[0] != dx:
                    continue
                x = rpack[XOFF.index(off), pair]
                keep = None
                shift = 0
                if off[1]:
                    x = pltpu.roll(x, 1 if off[1] < 0 else PTS - 1, 0)
                    keep = ((prow == 0) & (pye == 0)) if off[1] < 0 else ((prow == ORDER) & (pye == yel - 1))
                    shift += -(yel - 1) if off[1] < 0 else yel - 1
                if off[2]:
                    t = (pz == 0) if off[2] < 0 else (pz == planes - 1)
                    keep = t if keep is None else keep & t
                    shift += (-(planes - 1) if off[2] < 0 else planes - 1) * yel
                if shift:
                    x = pltpu.roll(x, shift % cols, 1)
                ok = there(off)
                keep = jnp.broadcast_to(ok, pshape) if keep is None else keep & ok
                acc = acc + jnp.where(keep, x, 0.0)
            halo[s][pair] = acc
    for s in range(2):
        for pair in range(2):
            pack_halo = halo[s][pair]
            flux[0, 0, s * 2 + pair, 0:PTS, :] = pack_halo

    def y_halo(c, s, dy):
        acc = jnp.where(there((0, dy, 0)), ryface[YOFF.index((0, dy, 0)), c], 0.0)
        z1 = lax.broadcasted_iota(jnp.int32, (planes, cols), 0)
        for dz, z in ((-1, 0), (1, planes - 1)):
            off = (0, dy, dz)
            acc = acc + jnp.where((z1 == z) & there(off), ryz[YZOFF.index(off), c], 0.0)
        return acc

    edge = ((lane == 0) & (ix == 0)) | ((lane == cols - 1) & (ix == nx - 1))
    edge = edge | ((k_at == 0) & (ye_at == 0) & (iy == 0))
    edge = edge | ((k_at == ORDER) & (ye_at == yel - 1) & (iy == ny - 1))

    def full(c, store):
        pair, base = c // 2, (c % 2) * half
        ylo = y_halo(c, 0, -1)
        yhi = y_halo(c, 1, 1)
        low = flux[0, 0, pair, 0:PTS, :]
        high = flux[0, 0, 2 + pair, 0:PTS, :]
        for e in range(layers):
            at = pl.ds(e * PTS, PTS)
            hit = lane == base + (e * PTS + z_at) * yel + ye_at
            wide = jnp.concatenate(
                [
                    jnp.where(hit, high[None, None], 0.0).reshape(PTS * rows, cols),
                    jnp.where(hit, low[None, None], 0.0).reshape(PTS * rows, cols),
                ],
                axis=1,
            )
            hi, lo = split(wide)
            x = (dot(hi, put_ref[...]) + dot(lo, put_ref[...])).reshape(four)
            x = x + field[c, at].reshape(four)
            yl = ylo[e * PTS:(e + 1) * PTS][:, None, None, :]
            yh = yhi[e * PTS:(e + 1) * PTS][:, None, None, :]
            x = x + jnp.where((k_at == 0) & (ye_at == 0), yl, 0.0)
            x = x + jnp.where((k_at == ORDER) & (ye_at == yel - 1), yh, 0.0)
            out_edge = edge
            if e == 0:
                zl = jnp.where(there((0, 0, -1)), rzface[0, c], 0.0).reshape(1, yel, PTS, cols)
                x = x + jnp.where(z_at == 0, zl, 0.0)
                out_edge = out_edge | ((z_at == 0) & (iz == 0))
            if e == layers - 1:
                zh = jnp.where(there((0, 0, 1)), rzface[1, c], 0.0).reshape(1, yel, PTS, cols)
                x = x + jnp.where(z_at == PTS - 1, zh, 0.0)
                out_edge = out_edge | ((z_at == PTS - 1) & (iz == nz - 1))
            store(at, jnp.where(out_edge, 0.0, x).reshape(PTS, rows, cols))

    def store_mass(at, x):
        m_out[at] = x

    full(3, store_mass)

    @pl.loop(0, 3)
    def _(c):
        def store(at, x):
            a_out[c, at] = x

        full(c, store)

    rest = parts.at[pl.ds(0, count - 1)]
    pltpu.make_async_copy(rest, rest, srecv).wait()
    total = jnp.sum(parts[...], axis=0)
    total = jnp.sum(total, axis=1, keepdims=True)
    s_out[0:2, :] = jnp.broadcast_to(total, (2, cols))
    s_out[2:3, :] = jnp.broadcast_to(total[1:2] / (2.0 * total[0:1]), (1, cols))

    for off in OFFS:
        @pl.when(there(off))
        def _(off=off):
            copy_to(off).wait_send()

    @pl.loop(1, count)
    def _(step):
        scalar_copy(step).wait_send()


def per_device(sizes, velocity, geometry, mass_weights):
    planes, rows, cols = mass_weights.shape
    f32 = jnp.float32
    count = sizes[0] * sizes[1] * sizes[2]
    vmem = pl.BlockSpec(memory_space=pltpu.VMEM)
    hbm = pl.BlockSpec(memory_space=pl.ANY)
    applied, mass, scalars = pl.pallas_call(
        functools.partial(kernel, sizes),
        out_shape=(
            jax.ShapeDtypeStruct(velocity.shape, f32),
            jax.ShapeDtypeStruct(mass_weights.shape, f32),
            jax.ShapeDtypeStruct((8, cols), f32),
        ),
        in_specs=[hbm] * 3 + [vmem] * 6,
        out_specs=(vmem, vmem, vmem),
        scratch_shapes=[
            pltpu.VMEM(velocity.shape, f32),
            pltpu.VMEM(geometry.shape, geometry.dtype),
            pltpu.VMEM(mass_weights.shape, mass_weights.dtype),
            pltpu.VMEM((3,) + velocity.shape, f32),
            pltpu.VMEM((4, planes, rows, cols), f32),
            pltpu.VMEM((2, 2, PTS, cols), f32),
            pltpu.VMEM((2, 4, planes, cols), f32),
            pltpu.VMEM((2, 2, 4, 1, cols), f32),
            pltpu.VMEM((len(XOFF), 2, PTS, cols), f32),
            pltpu.VMEM((2, 4, planes, cols), f32),
            pltpu.VMEM((2, 4, rows, cols), f32),
            pltpu.VMEM((len(YZOFF), 4, 1, cols), f32),
            pltpu.VMEM((2, cols), f32),
            pltpu.VMEM((count, 2, cols), f32),
            pltpu.SemaphoreType.DMA((3,)),
            pltpu.SemaphoreType.DMA((len(OFFS),)),
            pltpu.SemaphoreType.DMA((len(OFFS),)),
            pltpu.SemaphoreType.DMA,
            pltpu.SemaphoreType.DMA,
        ],
        compiler_params=pltpu.CompilerParams(
            collective_id=0, has_side_effects=True, vmem_limit_bytes=40 * 1024 * 1024
        ),
    )(velocity, geometry, mass_weights, *tables(rows, cols))
    residual = applied - scalars[2, 0] * mass[None] * velocity
    return residual, scalars[0, 0], scalars[1, 0]


def solution(mesh):
    sizes = tuple(mesh.shape[a] for a in AXES)
    in_specs = (P(None, "gz", "gy", "gx"), P(None, "gz", "gy", "gx"), P("gz", "gy", "gx"))
    out_specs = (P(None, "gz", "gy", "gx"), P(), P())
    return jax.shard_map(
        functools.partial(per_device, sizes),
        mesh=mesh, in_specs=in_specs, out_specs=out_specs, check_vma=False,
    )
```

time: 91.1 us -> 27.8 us (0.31)
  blocking collectives: 41.7 us -> 0 us
  Pallas kernels: 0 us -> 15.9 us
  starting transfers between devices: 15.4 us -> 0 us
  other arithmetic: 9.7 us -> 1.73 us
  matrix products: 7.95 us -> 0 us
  waiting for transfers between devices: 4.74 us -> 0 us
  between operations: 2.95 us -> 0.66 us
  local copies, waits for them, and re-layouts: 8.03 us -> 9.13 us
    psum x1 -> x0, blocking collectives: 41.7 us -> none  [per_device(): lax.psum((kinetic_part, enstrophy_part), ('gx', 'gy', 'gz'))]
    pallas_call x0 -> x1, Pallas kernels: none -> 15.9 us  [per_device(): pl.pallas_call(functools.partial(kernel, sizes), out_shape=(jax.ShapeDtyp...]
    ppermute x6 -> x0, starting transfers between devices: 15.4 us -> none  [the longest x3 11.5 us: padded_2(): lax.ppermute(lax.slice_in_dim(block, block.shape[dim] - width, None, axis...]
    dot_general x6 -> x0, matrix products: 7.95 us -> none  [the longest x2 3.5 us: derive(): return jnp.einsum('czyx,wy->czwx', source, block_table, precision=highest)]
    unnamed x20 -> x18, local copies, waits for them, and re-layouts: 1.65 us -> 8.61 us
    ppermute x6 -> x0, waiting for transfers between devices: 4.74 us -> none  [the longest x3 3.16 us: padded_2(): lax.ppermute(lax.slice_in_dim(block, 0, width, axis=dim), axis, backward)]
    add x3 -> x0, other arithmetic: 3.01 us -> none  [assemble_padded(): return result + jnp.where(position % points == 0, prev_val, 0.0)]
    ppermute x2 -> x0, local copies, waits for them, and re-layouts: 2.88 us -> none  [the longest x1 1.45 us: padded_2(): lax.ppermute(lax.slice_in_dim(block, block.shape[dim] - width, None, axis...]
  transfers between devices with their start and end apart: 6 -> 0, of which waited for: 3 -> 0; matrix products, arithmetic and copies ran while one was open for 3% -> 0% of each run, Pallas kernels for 0% -> 0%
where the time goes in v1:
time: 27.8 us; the launch traced here: 27.4 us
  Pallas kernels  15.9 us (57%)
  local copies, waits for them, and re-layouts  9.13 us (33%)
  other arithmetic  1.73 us (6%)
  between operations  0.66 us (2%)
    pallas_call x1, Pallas kernels, per_device(): pl.pallas_call(functools.partial(kernel, sizes), out_shape=(jax.ShapeDtyp...  15.9 us
    unnamed x18, local copies, waits for them, and re-layouts  8.61 us
    sub x1, other arithmetic, per_device(): residual = applied - scalars[2, 0] * mass[None] * velocity  1.07 us
    mul x1, other arithmetic, per_device(): residual = applied - scalars[2, 0] * mass[None] * velocity  0.66 us

profile of v1, /device:TPU:0, one launch (start us, length us, event | category | flops | bytes accessed | tf_op | source)
XLA Modules:
  0.0 27.4 jit_solution(7977630034506786846)
XLA Ops:
  0.6 0.0 copy-start
  0.6 1.1 %copy-done = f32[3,16,32,128]{3,2,1,0:T(8,128)S(1)} copy-done((f32[3,16,32,128]{3,2,1,0:T(8,128)S(1)}, f32[3,16,32,128]{3,2,1,0:T(8,128)}, u32[]{:S(2)}) %copy-start) | copy-done | bytes 786456
  1.8 0.0 copy-start.1
  1.8 1.1 %copy-done.1 = bf16[6,16,32,128]{3,2,1,0:T(8,128)(2,1)S(1)} copy-done((bf16[6,16,32,128]{3,2,1,0:T(8,128)(2,1)S(1)}, bf16[6,16,32,128]{3,2,1,0:T(8,128)(2,1)}, u32[]{:S(2)}) %copy-start.1) | copy-done | bytes 786456
  2.9 0.0 copy-start.2
  2.9 0.9 %copy-done.2 = bf16[2,256,256]{2,1,0:T(8,128)(2,1)S(1)} copy-done((bf16[2,256,256]{2,1,0:T(8,128)(2,1)S(1)}, bf16[2,256,256]{2,1,0:T(8,128)(2,1)}, u32[]{:S(2)}) %copy-start.2) | copy-done | bytes 262168
  3.8 0.0 copy-start.3
  3.9 0.9 %copy-done.3 = bf16[2,256,256]{2,1,0:T(8,128)(2,1)S(1)} copy-done((bf16[2,256,256]{2,1,0:T(8,128)(2,1)S(1)}, bf16[2,256,256]{2,1,0:T(8,128)(2,1)}, u32[]{:S(2)}) %copy-start.3) | copy-done | bytes 262168
  4.8 0.0 copy-start.4
  4.8 0.9 %copy-done.4 = bf16[16,32,128]{2,1,0:T(8,128)(2,1)S(1)} copy-done((bf16[16,32,128]{2,1,0:T(8,128)(2,1)S(1)}, bf16[16,32,128]{2,1,0:T(8,128)(2,1)}, u32[]{:S(2)}) %copy-start.4) | copy-done | bytes 131096
  5.7 0.0 copy-start.5
  5.7 0.9 %copy-done.5 = bf16[256,256]{1,0:T(8,128)(2,1)S(1)} copy-done((bf16[256,256]{1,0:T(8,128)(2,1)S(1)}, bf16[256,256]{1,0:T(8,128)(2,1)}, u32[]{:S(2)}) %copy-start.5) | copy-done | bytes 131096
  6.6 0.0 copy-start.6
  6.6 0.9 %copy-done.6 = bf16[256,256]{1,0:T(8,128)(2,1)S(1)} copy-done((bf16[256,256]{1,0:T(8,128)(2,1)S(1)}, bf16[256,256]{1,0:T(8,128)(2,1)}, u32[]{:S(2)}) %copy-start.6) | copy-done | bytes 131096
  7.5 0.0 copy-start.7
  7.5 0.9 %copy-done.7 = bf16[256,256]{1,0:T(8,128)(2,1)S(1)} copy-done((bf16[256,256]{1,0:T(8,128)(2,1)S(1)}, bf16[256,256]{1,0:T(8,128)(2,1)}, u32[]{:S(2)}) %copy-start.7) | copy-done | bytes 131096
  8.4 0.0 copy-start.8
  8.4 0.8 %copy-done.8 = bf16[256,128]{1,0:T(8,128)(2,1)S(1)} copy-done((bf16[256,128]{1,0:T(8,128)(2,1)S(1)}, bf16[256,128]{1,0:T(8,128)(2,1)}, u32[]{:S(2)}) %copy-start.8) | copy-done | bytes 65560
  9.3 15.9 %shard_map.112 = (f32[3,16,32,128]{3,2,1,0:T(8,128)S(1)}, f32[16,32,128]{2,1,0:T(8,128)S(1)}, f32[8,128]{1,0:T(8,128)S(1)}) custom-call(f32[3,16,32,128]{3,2,1,0:T(8,128)S(1)} %copy-done, bf16[6,16,32,128]{3,2,1,0:T(8,128)(2,1)S(1)} %copy-done.1, bf16[16,32,128]{2,1,0:T(8,128)(2,1)S(1)} %copy-done.4, bf16[256,256]{1,0:T(8,128)(2,1)S(1)} %copy-done.7, ...), custom_call_target="tpu_custom_call" | custom-call | tf_op jit(solution)/shard_map/pallas_call | solution.py:415
  25.2 0.5 %fusion = (f32[1,1]{1,0:T(1,128)}, f32[1,1]{1,0:T(1,128)}, f32[1,1]{1,0:T(1,128)}) fusion(f32[8,128]{1,0:T(8,128)S(1)} %get-tuple-element.7), kind=kLoop, calls=%fused_computation.2 | loop fusion | bytes 24 | tf_op jit(solution)/shard_map/slice | solution.py:450
  25.7 0.7 %broadcast_multiply_fusion = f32[16,32,128]{2,1,0:T(8,128)S(1)} fusion(f32[16,32,128]{2,1,0:T(8,128)S(1)} %get-tuple-element.8, f32[]{:T(128)} %bitcast), kind=kLoop, calls=%fused_computation.1 | loop fusion | flops 65536 | bytes 524292 | tf_op jit(solution)/shard_map/mul | solution.py:449
  26.4 1.1 %multiply_subtract_fusion = f32[3,16,32,128]{3,2,1,0:T(8,128)} fusion(f32[3,16,32,128]{3,2,1,0:T(8,128)S(1)} %get-tuple-element.6, f32[3,16,32,128]{3,2,1,0:T(8,128)S(1)} %copy-done, f32[16,32,128]{2,1,0:T(8,128)S(1)} %broadcast_multiply_fusion), kind=kLoop, calls=%fused_computation | loop fusion | flops 393216 | bytes 2621440 | tf_op jit(solution)/shard_map/sub | solution.py:449
Async XLA Ops:
  0.6 1.1 %copy-start = (f32[3,16,32,128]{3,2,1,0:T(8,128)S(1)}, f32[3,16,32,128]{3,2,1,0:T(8,128)}, u32[]{:S(2)}) copy-start(f32[3,16,32,128]{3,2,1,0:T(8,128)} %v_hbm.1) | copy-start | bytes 2359300
  1.8 1.1 %copy-start.1 = (bf16[6,16,32,128]{3,2,1,0:T(8,128)(2,1)S(1)}, bf16[6,16,32,128]{3,2,1,0:T(8,128)(2,1)}, u32[]{:S(2)}) copy-start(bf16[6,16,32,128]{3,2,1,0:T(8,128)(2,1)} %g_hbm.1) | copy-start | bytes 2359300
  2.9 0.9 %copy-start.2 = (bf16[2,256,256]{2,1,0:T(8,128)(2,1)S(1)}, bf16[2,256,256]{2,1,0:T(8,128)(2,1)}, u32[]{:S(2)}) copy-start(bf16[2,256,256]{2,1,0:T(8,128)(2,1)} %constant.15.clone.ty_ref) | copy-start | bytes 786436
  3.8 0.9 %copy-start.3 = (bf16[2,256,256]{2,1,0:T(8,128)(2,1)S(1)}, bf16[2,256,256]{2,1,0:T(8,128)(2,1)}, u32[]{:S(2)}) copy-start(bf16[2,256,256]{2,1,0:T(8,128)(2,1)} %constant.13.clone.dy_ref) | copy-start | bytes 786436
  4.8 0.9 %copy-start.4 = (bf16[16,32,128]{2,1,0:T(8,128)(2,1)S(1)}, bf16[16,32,128]{2,1,0:T(8,128)(2,1)}, u32[]{:S(2)}) copy-start(bf16[16,32,128]{2,1,0:T(8,128)(2,1)} %m_hbm.1) | copy-start | bytes 393220
  5.7 0.9 %copy-start.5 = (bf16[256,256]{1,0:T(8,128)(2,1)S(1)}, bf16[256,256]{1,0:T(8,128)(2,1)}, u32[]{:S(2)}) copy-start(bf16[256,256]{1,0:T(8,128)(2,1)} %constant.16.clone.pick_ref) | copy-start | bytes 393220
  6.6 0.9 %copy-start.6 = (bf16[256,256]{1,0:T(8,128)(2,1)S(1)}, bf16[256,256]{1,0:T(8,128)(2,1)}, u32[]{:S(2)}) copy-start(bf16[256,256]{1,0:T(8,128)(2,1)} %constant.14.clone.tx_ref) | copy-start | bytes 393220
  7.5 0.9 %copy-start.7 = (bf16[256,256]{1,0:T(8,128)(2,1)S(1)}, bf16[256,256]{1,0:T(8,128)(2,1)}, u32[]{:S(2)}) copy-start(bf16[256,256]{1,0:T(8,128)(2,1)} %constant.12.clone.dx_ref) | copy-start | bytes 393220
  8.4 0.8 %copy-start.8 = (bf16[256,128]{1,0:T(8,128)(2,1)S(1)}, bf16[256,128]{1,0:T(8,128)(2,1)}, u32[]{:S(2)}) copy-start(bf16[256,128]{1,0:T(8,128)(2,1)} %constant.17.clone.put_ref) | copy-start | bytes 196612

commit v2 on v1

--- a/solution.py
+++ b/solution.py
@@ -106,9 +106,9 @@
 
 def kernel(
     sizes,
-    v_hbm, g_hbm, m_hbm, dx_ref, dy_ref, tx_ref, ty_ref, pick_ref, put_ref,
-    a_out, m_out, s_out,
-    v, g, m, flux, field, pack, yface, yzrow, rpack, ryface, rzface, ryz, part, parts,
+    v_hbm, g_hbm, m_hbm, dx_hbm, dy_hbm, tx_hbm, ty_hbm, pick_hbm, put_hbm,
+    a_out, b_out, s_out,
+    v, g, m, dx_ref, dy_ref, tx_ref, ty_ref, pick_ref, put_ref, mfull, flux, field, pack, yface, yzrow, rpack, ryface, rzface, ryz, part, parts,
     in_sem, send_sem, recv_sem, ssend, srecv,
 ):
     nx, ny, nz = sizes
@@ -123,7 +123,12 @@
 
     loads = [
         pltpu.make_async_copy(src, dst, in_sem.at[k])
-        for k, (src, dst) in enumerate(((m_hbm, m), (v_hbm, v), (g_hbm, g)))
+        for k, (src, dst) in enumerate(
+            (
+                (m_hbm, m), (pick_hbm, pick_ref), (v_hbm, v), (g_hbm, g), (dx_hbm, dx_ref),
+                (dy_hbm, dy_ref), (tx_hbm, tx_ref), (ty_hbm, ty_ref), (put_hbm, put_ref),
+            )
+        )
     ]
     for c in loads:
         c.start()
@@ -186,12 +191,13 @@
 
     pack[...] = jnp.zeros(pack.shape, jnp.float32)
     loads[0].wait()
+    loads[1].wait()
     for e in range(layers):
         x = m[pl.ds(e * PTS, PTS)].astype(jnp.float32).reshape(PTS * rows, cols)
         field[3, pl.ds(e * PTS, PTS)] = assemble_xy(x).reshape(PTS, rows, cols)
     finish_channel(3)
-    loads[1].wait()
-    loads[2].wait()
+    for c in loads[2:]:
+        c.wait()
 
     def gradients(step, acc):
         kin, ens = acc
@@ -378,7 +384,7 @@
             store(at, jnp.where(out_edge, 0.0, x).reshape(PTS, rows, cols))
 
     def store_mass(at, x):
-        m_out[at] = x
+        mfull[at] = x
 
     full(3, store_mass)
 
@@ -386,6 +392,7 @@
     def _(c):
         def store(at, x):
             a_out[c, at] = x
+            b_out[c, at] = mfull[at] * v[c, at]
 
         full(c, store)
 
@@ -393,8 +400,7 @@
     pltpu.make_async_copy(rest, rest, srecv).wait()
     total = jnp.sum(parts[...], axis=0)
     total = jnp.sum(total, axis=1, keepdims=True)
-    s_out[0:2, :] = jnp.broadcast_to(total, (2, cols))
-    s_out[2:3, :] = jnp.broadcast_to(total[1:2] / (2.0 * total[0:1]), (1, cols))
+    s_out[...] = jnp.broadcast_to(total, (2, cols))
 
     for off in OFFS:
         @pl.when(there(off))
@@ -404,6 +410,27 @@
     @pl.loop(1, count)
     def _(step):
         scalar_copy(step).wait_send()
+
+
+def finish(a_ref, b_ref, s_ref, r_hbm, k_hbm, e_hbm, r, k, e, sem):
+    chunks = r.shape[0]
+    kin = s_ref[0:1, 0:1]
+    ens = s_ref[1:2, 0:1]
+    rayleigh = ens / (2.0 * kin)
+    k[...] = kin
+    e[...] = ens
+    outs = [
+        pltpu.make_async_copy(k, k_hbm, sem.at[chunks]),
+        pltpu.make_async_copy(e, e_hbm, sem.at[chunks + 1]),
+    ]
+    for c in range(chunks):
+        r[c] = a_ref[c] - rayleigh[None] * b_ref[c]
+        outs.append(pltpu.make_async_copy(r.at[c], r_hbm.at[c], sem.at[c]))
+        outs[-1].start()
+    outs[0].start()
+    outs[1].start()
+    for c in outs:
+        c.wait()
 
 
 def per_device(sizes, velocity, geometry, mass_weights):
@@ -411,20 +438,23 @@
     f32 = jnp.float32
     count = sizes[0] * sizes[1] * sizes[2]
     vmem = pl.BlockSpec(memory_space=pltpu.VMEM)
-    hbm = pl.BlockSpec(memory_space=pl.ANY)
-    applied, mass, scalars = pl.pallas_call(
+    hbm = pl.BlockSpec(memory_space=pltpu.HBM)
+    consts = tables(rows, cols)
+    applied, weighted, scalars = pl.pallas_call(
         functools.partial(kernel, sizes),
         out_shape=(
             jax.ShapeDtypeStruct(velocity.shape, f32),
-            jax.ShapeDtypeStruct(mass_weights.shape, f32),
-            jax.ShapeDtypeStruct((8, cols), f32),
+            jax.ShapeDtypeStruct(velocity.shape, f32),
+            jax.ShapeDtypeStruct((2, cols), f32),
         ),
-        in_specs=[hbm] * 3 + [vmem] * 6,
+        in_specs=[hbm] * 9,
         out_specs=(vmem, vmem, vmem),
         scratch_shapes=[
             pltpu.VMEM(velocity.shape, f32),
             pltpu.VMEM(geometry.shape, geometry.dtype),
             pltpu.VMEM(mass_weights.shape, mass_weights.dtype),
+            *[pltpu.VMEM(t.shape, t.dtype) for t in consts],
+            pltpu.VMEM(mass_weights.shape, f32),
             pltpu.VMEM((3,) + velocity.shape, f32),
             pltpu.VMEM((4, planes, rows, cols), f32),
             pltpu.VMEM((2, 2, PTS, cols), f32),
@@ -436,18 +466,31 @@
             pltpu.VMEM((len(YZOFF), 4, 1, cols), f32),
             pltpu.VMEM((2, cols), f32),
             pltpu.VMEM((count, 2, cols), f32),
-            pltpu.SemaphoreType.DMA((3,)),
+            pltpu.SemaphoreType.DMA((9,)),
             pltpu.SemaphoreType.DMA((len(OFFS),)),
             pltpu.SemaphoreType.DMA((len(OFFS),)),
             pltpu.SemaphoreType.DMA,
             pltpu.SemaphoreType.DMA,
         ],
         compiler_params=pltpu.CompilerParams(
-            collective_id=0, has_side_effects=True, vmem_limit_bytes=40 * 1024 * 1024
+            collective_id=0, has_side_effects=True, vmem_limit_bytes=32 * 1024 * 1024
         ),
-    )(velocity, geometry, mass_weights, *tables(rows, cols))
-    residual = applied - scalars[2, 0] * mass[None] * velocity
-    return residual, scalars[0, 0], scalars[1, 0]
+    )(*(pltpu.with_memory_space_constraint(t, pltpu.HBM) for t in (velocity, geometry, mass_weights, *consts)))
+    one = jax.ShapeDtypeStruct((1, 1), f32)
+    residual, kinetic, enstrophy = pl.pallas_call(
+        finish,
+        out_shape=(jax.ShapeDtypeStruct(velocity.shape, f32), one, one),
+        in_specs=[vmem] * 3,
+        out_specs=(hbm,) * 3,
+        scratch_shapes=[
+            pltpu.VMEM(velocity.shape, f32),
+            pltpu.VMEM((1, 1), f32),
+            pltpu.VMEM((1, 1), f32),
+            pltpu.SemaphoreType.DMA((velocity.shape[0] + 2,)),
+        ],
+        compiler_params=pltpu.CompilerParams(vmem_limit_bytes=8 * 1024 * 1024),
+    )(applied, weighted, scalars)
+    return residual, kinetic[0, 0], enstrophy[0, 0]
 
 
 def solution(mesh):

time: 27.8 us -> 17.5 us (0.63)
  local copies, waits for them, and re-layouts: 9.13 us -> 0 us
  other arithmetic: 1.73 us -> 0 us
  Pallas kernels: 15.9 us -> 16.7 us
    unnamed x18 -> x0, local copies, waits for them, and re-layouts: 8.61 us -> none
    sub x1 -> x0, other arithmetic: 1.07 us -> none  [per_device(): residual = applied - scalars[2, 0] * mass[None] * velocity]
    pallas_call x0 -> x1, Pallas kernels: none -> 1 us  [per_device(): pl.pallas_call(finish, out_shape=(jax.ShapeDtypeStruct(velocity.shape, f3...]
    mul x1 -> x0, other arithmetic: 0.66 us -> none  [per_device(): residual = applied - scalars[2, 0] * mass[None] * velocity]
    slice x1 -> x0, local copies, waits for them, and re-layouts: 0.52 us -> none  [per_device(): return (residual, scalars[0, 0], scalars[1, 0])]
where the time goes in v2:
time: 17.5 us; the launch traced here: 17.3 us
  Pallas kernels  16.7 us (95%)
  between operations  0.64 us (4%)
    pallas_call x1, Pallas kernels, per_device(): pl.pallas_call(functools.partial(kernel, sizes), out_shape=(jax.ShapeDtyp...  15.7 us
    pallas_call x1, Pallas kernels, per_device(): pl.pallas_call(finish, out_shape=(jax.ShapeDtypeStruct(velocity.shape, f3...  1 us

profile of v2, /device:TPU:0, one launch (start us, length us, event | category | flops | bytes accessed | tf_op | source)
XLA Modules:
  0.0 17.3 jit_solution(7465831903680119088)
XLA Ops:
  0.6 15.7 %shard_map.112 = (f32[3,16,32,128]{3,2,1,0:T(8,128)S(1)}, f32[3,16,32,128]{3,2,1,0:T(8,128)S(1)}, f32[2,128]{1,0:T(2,128)S(1)}) custom-call(f32[3,16,32,128]{3,2,1,0:T(8,128)} %v_hbm.1, bf16[6,16,32,128]{3,2,1,0:T(8,128)(2,1)} %g_hbm.1, bf16[16,32,128]{2,1,0:T(8,128)(2,1)} %m_hbm.1, bf16[256,256]{1,0:T(8,128)(2,1)} %constant.12.clone.dx_hbm, ...), custom_call_target="tpu_custom_call" | custom-call | tf_op jit(solution)/shard_map/pallas_call | solution.py:443
  16.3 1.0 %shard_map.113 = (f32[3,16,32,128]{3,2,1,0:T(8,128)}, f32[1,1]{1,0:T(1,128)}, f32[1,1]{1,0:T(1,128)}) custom-call(f32[3,16,32,128]{3,2,1,0:T(8,128)S(1)} %get-tuple-element.9.a_ref, f32[3,16,32,128]{3,2,1,0:T(8,128)S(1)} %get-tuple-element.10.b_ref, f32[2,128]{1,0:T(2,128)S(1)} %get-tuple-element.11.s_ref), custom_call_target="tpu_custom_call" | custom-call | tf_op jit(solution)/shard_map/pallas_call | solution.py:480

commit v3 on v2

--- a/solution.py
+++ b/solution.py
@@ -60,14 +60,15 @@
         out.append(np.block([[hi, lo], [hi, zero]]))
         hi, lo = split_np(np.kron(np.eye(PTS * rows // PTS, dtype=np.float32), mat))
         out.append(np.stack([hi, lo]))
-    pick = np.zeros((2 * cols, 2 * cols), np.float32)
-    for base in (0, cols):
-        pick[base, :cols] = 1.0
-        pick[base + cols - 1, cols:] = 1.0
+    pick = np.zeros((2 * PTS, 2 * cols), np.float32)
+    pick[0, [0, cols]] = 1.0
+    pick[1, [cols - 1, 2 * cols - 1]] = 1.0
     out.append(pick.astype(jnp.bfloat16))
-    put = np.zeros((2 * cols, cols), np.float32)
-    put[:cols, cols - 1] = 1.0
-    put[cols:, 0] = 1.0
+    put = np.zeros((16, 4 * cols), np.float32)
+    for c in range(4):
+        for base in (0, 8):
+            put[base + c, c * cols + cols - 1] = 1.0
+            put[base + 4 + c, c * cols] = 1.0
     out.append(put.astype(jnp.bfloat16))
     return [jnp.asarray(t) for t in out]
 
@@ -95,20 +96,28 @@
 
 
 def along_z(planes, mat):
-    out = []
-    for w in range(PTS):
-        acc = planes[0] * float(mat[w, 0])
-        for z in range(1, PTS):
-            acc = acc + planes[z] * float(mat[w, z])
-        out.append(acc)
-    return out
+    n = PTS // 2
+    mat = mat.astype(np.float64)
+    odd = [planes[j] - planes[ORDER - j] for j in range(n)]
+    even = [planes[j] + planes[ORDER - j] for j in range(n)]
+    low, high = [], []
+    for i in range(n):
+        p = q = None
+        for j in range(n):
+            t = odd[j] * float(0.5 * (mat[i, j] - mat[i, ORDER - j]))
+            u = even[j] * float(0.5 * (mat[i, j] + mat[i, ORDER - j]))
+            p = t if p is None else p + t
+            q = u if q is None else q + u
+        low.append(p + q)
+        high.append(p - q)
+    return low + high[::-1]
 
 
 def kernel(
     sizes,
     v_hbm, g_hbm, m_hbm, dx_hbm, dy_hbm, tx_hbm, ty_hbm, pick_hbm, put_hbm,
     a_out, b_out, s_out,
-    v, g, m, dx_ref, dy_ref, tx_ref, ty_ref, pick_ref, put_ref, mfull, flux, field, pack, yface, yzrow, rpack, ryface, rzface, ryz, part, parts,
+    v, g, m, dx_ref, dy_ref, tx_ref, ty_ref, pick_ref, put_ref, flux, field, pack, yface, yzrow, rpack, ryface, rzface, ryz, part, parts, zface, keep, halo,
     in_sem, send_sem, recv_sem, ssend, srecv,
 ):
     nx, ny, nz = sizes
@@ -143,26 +152,36 @@
     def _(step):
         pl.semaphore_signal(barrier, inc=1, device_id=peer_id(step), device_id_type=MESH)
 
+    n_rows = PTS * rows
     four = (PTS, yel, PTS, cols)
-    ye_at = lax.broadcasted_iota(jnp.int32, four, 1)
-    k_at = lax.broadcasted_iota(jnp.int32, four, 2)
-    z_at = lax.broadcasted_iota(jnp.int32, four, 0)
-    lane = lax.broadcasted_iota(jnp.int32, four, 3)
-    lane2 = lax.broadcasted_iota(jnp.int32, (PTS * rows, cols), 1)
-    row2 = lax.broadcasted_iota(jnp.int32, (PTS * rows, cols), 0)
+    flat8 = (1, 1, PTS, cols)
+    lane = lax.broadcasted_iota(jnp.int32, flat8, 3)
+    k_at = lax.broadcasted_iota(jnp.int32, flat8, 2)
+
+    def unit(mask):
+        return jnp.where(mask, 1.0, 0.0).astype(jnp.float32)
+
+    x_next = unit((lane % PTS == ORDER) & (lane < cols - 1))
+    x_prev = unit((lane % PTS == 0) & (lane > 0))
+    y_last = unit(k_at == ORDER)
+    y_first = unit(k_at == 0)
 
     def assemble_xy(x):
-        n = PTS * rows
-        x = (
-            x
-            + jnp.where((lane2 % PTS == ORDER) & (lane2 < cols - 1), pltpu.roll(x, cols - 1, 1), 0.0)
-            + jnp.where((lane2 % PTS == 0) & (lane2 > 0), pltpu.roll(x, 1, 1), 0.0)
-        )
-        return (
-            x
-            + jnp.where((row2 % PTS == ORDER) & (row2 % rows < rows - 1), pltpu.roll(x, n - 1, 0), 0.0)
-            + jnp.where((row2 % PTS == 0) & (row2 % rows > 0), pltpu.roll(x, 1, 0), 0.0)
-        )
+        up = pltpu.roll(x, cols - 1, 1).reshape(four)
+        down = pltpu.roll(x, 1, 1).reshape(four)
+        x = x.reshape(four) + up * x_next + down * x_prev
+        flat = x.reshape(PTS * yel, PTS, cols)
+        up = pltpu.roll(flat, PTS - 1, 1).reshape(four)
+        down = pltpu.roll(flat, 1, 1).reshape(four)
+        out = []
+        for y in range(yel):
+            t = x[:, y:y + 1]
+            if y < yel - 1:
+                t = t + up[:, y + 1:y + 2] * y_last
+            if y > 0:
+                t = t + down[:, y - 1:y] * y_first
+            out.append(t)
+        return jnp.concatenate(out, axis=1).reshape(PTS, rows, cols)
 
     def finish_channel(c):
         for e in range(1, layers):
@@ -171,30 +190,37 @@
             both = low + high
             field[c, e * PTS - 1] = both
             field[c, e * PTS] = both
-        lo_acc = jnp.zeros((PTS, cols), jnp.float32)
-        hi_acc = jnp.zeros((PTS, cols), jnp.float32)
-        base = (c % 2) * half
         for e in range(layers):
-            x = field[c, pl.ds(e * PTS, PTS)].reshape(PTS * rows, cols)
-            r = dot(jnp.concatenate(split(x), axis=1), pick_ref[...])
-            hit = lane == base + (e * PTS + z_at) * yel + ye_at
-            lo_acc = lo_acc + jnp.sum(jnp.where(hit, r[:, :cols].reshape(four), 0.0), axis=(0, 1))
-            hi_acc = hi_acc + jnp.sum(jnp.where(hit, r[:, cols:].reshape(four), 0.0), axis=(0, 1))
-        pair = c // 2
-        pack[0, pair] = pack[0, pair] + lo_acc
-        pack[1, pair] = pack[1, pair] + hi_acc
+            x = field[c, pl.ds(e * PTS, PTS)].reshape(n_rows, cols)
+            r = lax.dot_general(
+                pick_ref[...], jnp.concatenate(split(x), axis=1), (((1,), (1,)), ((), ())),
+                preferred_element_type=jnp.float32,
+            )
+            for s in range(2):
+                pack[s, pl.ds(c, 1), pl.ds(e * n_rows, n_rows)] = r[s:s + 1]
         for side, y in ((0, 0), (1, rows - 1)):
             face = field[c, :, y, :]
             yface[side, c] = face
             yzrow[side, 0, c] = face[0:1]
             yzrow[side, 1, c] = face[planes - 1:planes]
-
-    pack[...] = jnp.zeros(pack.shape, jnp.float32)
+        zface[0, c] = field[c, 0]
+        zface[1, c] = field[c, planes - 1]
+
+    inner_x = unit(((lane > 0) | (ix > 0)) & ((lane < cols - 1) | (ix < nx - 1))).reshape(1, PTS, cols)
+    z3 = lax.broadcasted_iota(jnp.int32, (planes, 1, cols), 0)
+    inner_z = unit(((z3 > 0) | (iz > 0)) & ((z3 < planes - 1) | (iz < nz - 1)))
+    for y in range(yel):
+        w = inner_x
+        if y == 0:
+            w = w * unit((k_at > 0) | (iy > 0)).reshape(1, PTS, cols)
+        if y == yel - 1:
+            w = w * unit((k_at < ORDER) | (iy < ny - 1)).reshape(1, PTS, cols)
+        keep[:, y * PTS:(y + 1) * PTS, :] = w * inner_z
     loads[0].wait()
     loads[1].wait()
     for e in range(layers):
         x = m[pl.ds(e * PTS, PTS)].astype(jnp.float32).reshape(PTS * rows, cols)
-        field[3, pl.ds(e * PTS, PTS)] = assemble_xy(x).reshape(PTS, rows, cols)
+        field[3, pl.ds(e * PTS, PTS)] = assemble_xy(x)
     finish_channel(3)
     for c in loads[2:]:
         c.wait()
@@ -250,7 +276,7 @@
             ft = flux[2, c, at]
             x = along_x(split(fr), tx_ref[...]) + along_y(split(fs), ty_ref[0], ty_ref[1])
             z = jnp.stack(along_z([ft[k] for k in range(PTS)], d.T))
-            field[c, at] = assemble_xy(x + z.reshape(x.shape)).reshape(PTS, rows, cols)
+            field[c, at] = assemble_xy(x + z.reshape(x.shape))
         finish_channel(c)
 
     here = (ix, iy, iz)
@@ -277,8 +303,7 @@
         elif off[1]:
             src, dst = yface.at[side(off[1])], ryface.at[YOFF.index(opp)]
         else:
-            plane = 0 if off[2] < 0 else planes - 1
-            src, dst = field.at[:, plane], rzface.at[ZOFF.index(opp)]
+            src, dst = zface.at[side(off[2])], rzface.at[ZOFF.index(opp)]
         return pltpu.make_async_remote_copy(
             src_ref=src, dst_ref=dst, send_sem=send_sem.at[n], recv_sem=recv_sem.at[slot],
             device_id={a: i + o for a, i, o in zip(AXES, here, off)}, device_id_type=MESH,
@@ -303,98 +328,56 @@
                 dst = rzface.at[ZOFF.index(off)]
             pltpu.make_async_copy(dst, dst, recv_sem.at[n]).wait()
 
-    pshape = (PTS, cols)
-    plane_lane = lax.broadcasted_iota(jnp.int32, pshape, 1)
-    prow = lax.broadcasted_iota(jnp.int32, pshape, 0)
-    pz = (plane_lane % half) // yel
-    pye = plane_lane % yel
-    halo = [[None, None], [None, None]]
-    for s, dx in ((0, -1), (1, 1)):
-        for pair in range(2):
-            acc = jnp.zeros(pshape, jnp.float32)
-            for off in XOFF:
-                if off[0] != dx:
-                    continue
-                x = rpack[XOFF.index(off), pair]
-                keep = None
-                shift = 0
-                if off[1]:
-                    x = pltpu.roll(x, 1 if off[1] < 0 else PTS - 1, 0)
-                    keep = ((prow == 0) & (pye == 0)) if off[1] < 0 else ((prow == ORDER) & (pye == yel - 1))
-                    shift += -(yel - 1) if off[1] < 0 else yel - 1
-                if off[2]:
-                    t = (pz == 0) if off[2] < 0 else (pz == planes - 1)
-                    keep = t if keep is None else keep & t
-                    shift += (-(planes - 1) if off[2] < 0 else planes - 1) * yel
-                if shift:
-                    x = pltpu.roll(x, shift % cols, 1)
-                ok = there(off)
-                keep = jnp.broadcast_to(ok, pshape) if keep is None else keep & ok
-                acc = acc + jnp.where(keep, x, 0.0)
-            halo[s][pair] = acc
-    for s in range(2):
-        for pair in range(2):
-            pack_halo = halo[s][pair]
-            flux[0, 0, s * 2 + pair, 0:PTS, :] = pack_halo
-
-    def y_halo(c, s, dy):
-        acc = jnp.where(there((0, dy, 0)), ryface[YOFF.index((0, dy, 0)), c], 0.0)
-        z1 = lax.broadcasted_iota(jnp.int32, (planes, cols), 0)
-        for dz, z in ((-1, 0), (1, planes - 1)):
-            off = (0, dy, dz)
-            acc = acc + jnp.where((z1 == z) & there(off), ryz[YZOFF.index(off), c], 0.0)
-        return acc
-
-    edge = ((lane == 0) & (ix == 0)) | ((lane == cols - 1) & (ix == nx - 1))
-    edge = edge | ((k_at == 0) & (ye_at == 0) & (iy == 0))
-    edge = edge | ((k_at == ORDER) & (ye_at == yel - 1) & (iy == ny - 1))
-
-    def full(c, store):
-        pair, base = c // 2, (c % 2) * half
-        ylo = y_halo(c, 0, -1)
-        yhi = y_halo(c, 1, 1)
-        low = flux[0, 0, pair, 0:PTS, :]
-        high = flux[0, 0, 2 + pair, 0:PTS, :]
-        for e in range(layers):
-            at = pl.ds(e * PTS, PTS)
-            hit = lane == base + (e * PTS + z_at) * yel + ye_at
-            wide = jnp.concatenate(
-                [
-                    jnp.where(hit, high[None, None], 0.0).reshape(PTS * rows, cols),
-                    jnp.where(hit, low[None, None], 0.0).reshape(PTS * rows, cols),
-                ],
-                axis=1,
-            )
-            hi, lo = split(wide)
-            x = (dot(hi, put_ref[...]) + dot(lo, put_ref[...])).reshape(four)
-            x = x + field[c, at].reshape(four)
-            yl = ylo[e * PTS:(e + 1) * PTS][:, None, None, :]
-            yh = yhi[e * PTS:(e + 1) * PTS][:, None, None, :]
-            x = x + jnp.where((k_at == 0) & (ye_at == 0), yl, 0.0)
-            x = x + jnp.where((k_at == ORDER) & (ye_at == yel - 1), yh, 0.0)
-            out_edge = edge
-            if e == 0:
-                zl = jnp.where(there((0, 0, -1)), rzface[0, c], 0.0).reshape(1, yel, PTS, cols)
-                x = x + jnp.where(z_at == 0, zl, 0.0)
-                out_edge = out_edge | ((z_at == 0) & (iz == 0))
-            if e == layers - 1:
-                zh = jnp.where(there((0, 0, 1)), rzface[1, c], 0.0).reshape(1, yel, PTS, cols)
-                x = x + jnp.where(z_at == PTS - 1, zh, 0.0)
-                out_edge = out_edge | ((z_at == PTS - 1) & (iz == nz - 1))
-            store(at, jnp.where(out_edge, 0.0, x).reshape(PTS, rows, cols))
-
-    def store_mass(at, x):
-        mfull[at] = x
-
-    full(3, store_mass)
-
-    @pl.loop(0, 3)
-    def _(c):
-        def store(at, x):
-            a_out[c, at] = x
-            b_out[c, at] = mfull[at] * v[c, at]
-
-        full(c, store)
+    total_rows = planes * rows
+    pshape = (4, total_rows)
+    place = lax.broadcasted_iota(jnp.int32, (1, total_rows), 1)
+    for s, dx in ((0, 1), (1, -1)):
+        acc = jnp.zeros(pshape, jnp.float32)
+        for off in XOFF:
+            if off[0] != dx:
+                continue
+            x = rpack[XOFF.index(off)]
+            hit = place >= 0
+            shift = 0
+            if off[1]:
+                hit = hit & (place % rows == (0 if off[1] < 0 else rows - 1))
+                shift += off[1] * (rows - 1)
+            if off[2]:
+                hit = hit & (place // rows == (0 if off[2] < 0 else planes - 1))
+                shift += off[2] * (planes - 1) * rows
+            if shift:
+                x = pltpu.roll(x, shift % total_rows, 1)
+            acc = acc + jnp.where(jnp.broadcast_to(hit & there(off), pshape), x, 0.0)
+        hi, lo = split(acc)
+        halo[s * 4:s * 4 + 4, :] = hi.astype(jnp.float32)
+        halo[8 + s * 4:12 + s * 4, :] = lo.astype(jnp.float32)
+
+    z1 = lax.broadcasted_iota(jnp.int32, (planes, cols), 0)
+
+    def add_yz(c):
+        for dy, y in ((-1, 0), (1, rows - 1)):
+            acc = jnp.where(there((0, dy, 0)), ryface[YOFF.index((0, dy, 0)), c], 0.0)
+            for dz, z in ((-1, 0), (1, planes - 1)):
+                off = (0, dy, dz)
+                acc = acc + jnp.where((z1 == z) & there(off), ryz[YZOFF.index(off), c], 0.0)
+            field[c, :, y, :] = field[c, :, y, :] + acc
+        for k, (dz, z) in enumerate(((-1, 0), (1, planes - 1))):
+            field[c, z] = field[c, z] + jnp.where(there((0, 0, dz)), rzface[k, c], 0.0)
+
+    for c in range(4):
+        add_yz(c)
+    halos = halo[...].astype(jnp.bfloat16)
+    for e in range(layers):
+        at = pl.ds(e * PTS, PTS)
+        x = lax.dot_general(
+            halos[:, e * n_rows:(e + 1) * n_rows], put_ref[...], (((0,), (0,)), ((), ())),
+            preferred_element_type=jnp.float32,
+        )
+        w = keep[at]
+        mass = (field[3, at] + x[:, 3 * cols:].reshape(PTS, rows, cols)) * w
+        for c in range(3):
+            a_out[c, at] = (field[c, at] + x[:, c * cols:(c + 1) * cols].reshape(PTS, rows, cols)) * w
+            b_out[c, at] = mass * v[c, at]
 
     rest = parts.at[pl.ds(0, count - 1)]
     pltpu.make_async_copy(rest, rest, srecv).wait()
@@ -454,18 +437,20 @@
             pltpu.VMEM(geometry.shape, geometry.dtype),
             pltpu.VMEM(mass_weights.shape, mass_weights.dtype),
             *[pltpu.VMEM(t.shape, t.dtype) for t in consts],
-            pltpu.VMEM(mass_weights.shape, f32),
             pltpu.VMEM((3,) + velocity.shape, f32),
             pltpu.VMEM((4, planes, rows, cols), f32),
-            pltpu.VMEM((2, 2, PTS, cols), f32),
+            pltpu.VMEM((2, 4, planes * rows), f32),
             pltpu.VMEM((2, 4, planes, cols), f32),
             pltpu.VMEM((2, 2, 4, 1, cols), f32),
-            pltpu.VMEM((len(XOFF), 2, PTS, cols), f32),
+            pltpu.VMEM((len(XOFF), 4, planes * rows), f32),
             pltpu.VMEM((2, 4, planes, cols), f32),
             pltpu.VMEM((2, 4, rows, cols), f32),
             pltpu.VMEM((len(YZOFF), 4, 1, cols), f32),
             pltpu.VMEM((2, cols), f32),
             pltpu.VMEM((count, 2, cols), f32),
+            pltpu.VMEM((2, 4, rows, cols), f32),
+            pltpu.VMEM(mass_weights.shape, f32),
+            pltpu.VMEM((16, planes * rows), f32),
             pltpu.SemaphoreType.DMA((9,)),
             pltpu.SemaphoreType.DMA((len(OFFS),)),
             pltpu.SemaphoreType.DMA((len(OFFS),)),

time: 17.5 us -> 16.4 us (0.937)
  Pallas kernels: 16.7 us -> 15.6 us
    pallas_call x1, Pallas kernels: 15.7 us -> 14.6 us  [per_device(): pl.pallas_call(functools.partial(kernel, sizes), out_shape=(jax.ShapeDtyp...]
where the time goes in v3:
time: 16.4 us; the launch traced here: 16.3 us
  Pallas kernels  15.6 us (95%)
  between operations  0.64 us (4%)
    pallas_call x1, Pallas kernels, per_device(): pl.pallas_call(functools.partial(kernel, sizes), out_shape=(jax.ShapeDtyp...  14.6 us
    pallas_call x1, Pallas kernels, per_device(): pl.pallas_call(finish, out_shape=(jax.ShapeDtypeStruct(velocity.shape, f3...  1 us

profile of v3, /device:TPU:0, one launch (start us, length us, event | category | flops | bytes accessed | tf_op | source)
XLA Modules:
  0.0 16.3 jit_solution(2907399543484605235)
XLA Ops:
  0.6 14.6 %shard_map.112 = (f32[3,16,32,128]{3,2,1,0:T(8,128)S(1)}, f32[3,16,32,128]{3,2,1,0:T(8,128)S(1)}, f32[2,128]{1,0:T(2,128)S(1)}) custom-call(f32[3,16,32,128]{3,2,1,0:T(8,128)} %v_hbm.1, bf16[6,16,32,128]{3,2,1,0:T(8,128)(2,1)} %g_hbm.1, bf16[16,32,128]{2,1,0:T(8,128)(2,1)} %m_hbm.1, bf16[256,256]{1,0:T(8,128)(2,1)} %constant.12.clone.dx_hbm, ...), custom_call_target="tpu_custom_call" | custom-call | tf_op jit(solution)/shard_map/pallas_call | solution.py:426
  15.3 1.0 %shard_map.113 = (f32[3,16,32,128]{3,2,1,0:T(8,128)}, f32[1,1]{1,0:T(1,128)}, f32[1,1]{1,0:T(1,128)}) custom-call(f32[3,16,32,128]{3,2,1,0:T(8,128)S(1)} %get-tuple-element.9.a_ref, f32[3,16,32,128]{3,2,1,0:T(8,128)S(1)} %get-tuple-element.10.b_ref, f32[2,128]{1,0:T(2,128)S(1)} %get-tuple-element.11.s_ref), custom_call_target="tpu_custom_call" | custom-call | tf_op jit(solution)/shard_map/pallas_call | solution.py:465

commit v4 on v3

--- a/solution.py
+++ b/solution.py
@@ -16,8 +16,8 @@
 XOFF = [o for o in itertools.product((-1, 0, 1), repeat=3) if o[0] != 0]
 YZOFF = [o for o in itertools.product((-1, 0, 1), repeat=3) if o[0] == 0 and o[1] != 0 and o[2] != 0]
 YOFF = [(0, -1, 0), (0, 1, 0)]
-ZOFF = [(0, 0, -1), (0, 0, 1)]
-OFFS = sorted(XOFF + YZOFF + YOFF + ZOFF, key=lambda o: -sum(map(abs, o)))
+FACES = YOFF + [(0, 0, -1), (0, 0, 1)]
+OFFS = sorted(XOFF + YZOFF, key=lambda o: -sum(map(abs, o)))
 
 
 def gll_derivative(poly_order):
@@ -118,7 +118,7 @@
     v_hbm, g_hbm, m_hbm, dx_hbm, dy_hbm, tx_hbm, ty_hbm, pick_hbm, put_hbm,
     a_out, b_out, s_out,
     v, g, m, dx_ref, dy_ref, tx_ref, ty_ref, pick_ref, put_ref, flux, field, pack, yface, yzrow, rpack, ryface, rzface, ryz, part, parts, zface, keep, halo,
-    in_sem, send_sem, recv_sem, ssend, srecv,
+    in_sem, send_sem, recv_sem, ssend, srecv, fsend, frecv,
 ):
     nx, ny, nz = sizes
     count = nx * ny * nz
@@ -146,11 +146,26 @@
         p = lax.rem(me + step, count)
         return {"gx": p // (ny * nz), "gy": lax.rem(p // nz, ny), "gz": lax.rem(p, nz)}
 
+    def ring(i, n):
+        out = [i]
+        for _ in range(n - 1):
+            t = out[-1] + 1
+            out.append(jnp.where(t == n, 0, t))
+        return out
+
+    def for_peers(act):
+        if count > 64:
+            pl.loop(1, count)(lambda step: act(peer_id(step)))
+            return
+        xs, ys, zs = (ring(i, n) for i, n in zip((ix, iy, iz), sizes))
+        for x, y, z in itertools.product(range(nx), range(ny), range(nz)):
+            if x or y or z:
+                act({"gx": xs[x], "gy": ys[y], "gz": zs[z]})
+
     barrier = pltpu.get_barrier_semaphore()
-
-    @pl.loop(1, count)
-    def _(step):
-        pl.semaphore_signal(barrier, inc=1, device_id=peer_id(step), device_id_type=MESH)
+    for_peers(
+        lambda to: pl.semaphore_signal(barrier, inc=1, device_id=to, device_id_type=MESH)
+    )
 
     n_rows = PTS * rows
     four = (PTS, yel, PTS, cols)
@@ -206,6 +221,60 @@
         zface[0, c] = field[c, 0]
         zface[1, c] = field[c, planes - 1]
 
+    total_rows = planes * rows
+    here = (ix, iy, iz)
+
+    def there(off):
+        ok = None
+        for o, i, n in zip(off, here, sizes):
+            if o:
+                t = (i > 0) if o < 0 else (i < n - 1)
+                ok = t if ok is None else ok & t
+        return ok
+
+    def side(o):
+        return (o + 1) // 2
+
+    def target(off):
+        return {a: i + o for a, i, o in zip(AXES, here, off)}
+
+    def part_of(dz):
+        width = total_rows // layers // 2
+        width = width if width % 128 == 0 else total_rows
+        if dz == 0:
+            return pl.ds(0, total_rows)
+        return pl.ds(0 if dz < 0 else total_rows - width, width)
+
+    def landing(off):
+        if off[0]:
+            return rpack.at[XOFF.index(off), :, part_of(-off[2])]
+        return ryz.at[YZOFF.index(off)]
+
+    def copy_to(off):
+        opp = tuple(-o for o in off)
+        if off[0]:
+            src = pack.at[side(off[0]), :, part_of(off[2])]
+        else:
+            src = yzrow.at[side(off[1]), side(off[2])]
+        return pltpu.make_async_remote_copy(
+            src_ref=src, dst_ref=landing(opp), send_sem=send_sem.at[OFFS.index(off)],
+            recv_sem=recv_sem.at[OFFS.index(opp)], device_id=target(off), device_id_type=MESH,
+        )
+
+    def face_copy(off, c):
+        k, opp = FACES.index(off), FACES.index(tuple(-o for o in off))
+        src, dst = (yface, ryface) if off[1] else (zface, rzface)
+        return pltpu.make_async_remote_copy(
+            src_ref=src.at[k % 2, c], dst_ref=dst.at[opp % 2, c], send_sem=fsend.at[k, c],
+            recv_sem=frecv.at[opp, c], device_id=target(off), device_id_type=MESH,
+        )
+
+    def send_faces(c):
+        for off in FACES[::-1]:
+            @pl.when(there(off))
+            def _(off=off):
+                face_copy(off, c).start()
+
     inner_x = unit(((lane > 0) | (ix > 0)) & ((lane < cols - 1) | (ix < nx - 1))).reshape(1, PTS, cols)
     z3 = lax.broadcasted_iota(jnp.int32, (planes, 1, cols), 0)
     inner_z = unit(((z3 > 0) | (iz > 0)) & ((z3 < planes - 1) | (iz < nz - 1)))
@@ -225,30 +294,30 @@
     for c in loads[2:]:
         c.wait()
 
-    def gradients(step, acc):
+    def gradients(e, acc):
         kin, ens = acc
-        c = step // layers
-        at = pl.ds(pl.multiple_of((step % layers) * PTS, PTS), PTS)
-        block = v[c, at]
-        flat = block.reshape(PTS * rows, cols)
+        at = pl.ds(pl.multiple_of(e * PTS, PTS), PTS)
         mass = m[at].astype(jnp.float32)
-        kin = kin + jnp.sum((mass * block * block).reshape(-1, PTS, cols), axis=0)
-        pair = split(flat)
-        gr = along_x(pair, dx_ref[...]).reshape(block.shape)
-        gs = along_y(pair, dy_ref[0], dy_ref[1]).reshape(block.shape)
-        gt = jnp.stack(along_z([block[z] for z in range(PTS)], d))
         g0, g1, g2, g3, g4, g5 = (g[k, at].astype(jnp.float32) for k in range(6))
-        fr = g0 * gr + g3 * gs + g4 * gt
-        fs = g3 * gr + g1 * gs + g5 * gt
-        ft = g4 * gr + g5 * gs + g2 * gt
-        ens = ens + jnp.sum((gr * fr + gs * fs + gt * ft).reshape(-1, PTS, cols), axis=0)
-        flux[0, c, at] = fr
-        flux[1, c, at] = fs
-        flux[2, c, at] = ft
+        for c in range(3):
+            block = v[c, at]
+            flat = block.reshape(PTS * rows, cols)
+            kin = kin + jnp.sum((mass * block * block).reshape(-1, PTS, cols), axis=0)
+            pair = split(flat)
+            gr = along_x(pair, dx_ref[...]).reshape(block.shape)
+            gs = along_y(pair, dy_ref[0], dy_ref[1]).reshape(block.shape)
+            gt = jnp.stack(along_z([block[z] for z in range(PTS)], d))
+            fr = g0 * gr + g3 * gs + g4 * gt
+            fs = g3 * gr + g1 * gs + g5 * gt
+            ft = g4 * gr + g5 * gs + g2 * gt
+            ens = ens + jnp.sum((gr * fr + gs * fs + gt * ft).reshape(-1, PTS, cols), axis=0)
+            flux[0, c, at] = fr
+            flux[1, c, at] = fs
+            flux[2, c, at] = ft
         return kin, ens
 
     zero = jnp.zeros((PTS, cols), jnp.float32)
-    kin, ens = lax.fori_loop(0, 3 * layers, gradients, (zero, zero))
+    kin, ens = lax.fori_loop(0, layers, gradients, (zero, zero))
     mine = jnp.concatenate(
         [jnp.sum(kin, 0, keepdims=True) * 0.5, jnp.sum(ens, 0, keepdims=True)], axis=0
     )
@@ -257,15 +326,14 @@
 
     pl.semaphore_wait(barrier, count - 1)
 
-    def scalar_copy(step):
+    def scalar_copy(to):
         return pltpu.make_async_remote_copy(
             src_ref=part, dst_ref=parts.at[me], send_sem=ssend, recv_sem=srecv,
-            device_id=peer_id(step), device_id_type=MESH,
+            device_id=to, device_id_type=MESH,
         )
 
-    @pl.loop(1, count)
-    def _(step):
-        scalar_copy(step).start()
+    for_peers(lambda to: scalar_copy(to).start())
+    send_faces(3)
 
     @pl.loop(0, 3)
     def _(c):
@@ -278,36 +346,7 @@
             z = jnp.stack(along_z([ft[k] for k in range(PTS)], d.T))
             field[c, at] = assemble_xy(x + z.reshape(x.shape))
         finish_channel(c)
-
-    here = (ix, iy, iz)
-
-    def there(off):
-        ok = None
-        for o, i, n in zip(off, here, sizes):
-            if o:
-                t = (i > 0) if o < 0 else (i < n - 1)
-                ok = t if ok is None else ok & t
-        return ok
-
-    def side(o):
-        return (o + 1) // 2
-
-    def copy_to(off):
-        n = OFFS.index(off)
-        opp = tuple(-o for o in off)
-        slot = OFFS.index(opp)
-        if off[0]:
-            src, dst = pack.at[side(off[0])], rpack.at[XOFF.index(opp)]
-        elif off[1] and off[2]:
-            src, dst = yzrow.at[side(off[1]), side(off[2])], ryz.at[YZOFF.index(opp)]
-        elif off[1]:
-            src, dst = yface.at[side(off[1])], ryface.at[YOFF.index(opp)]
-        else:
-            src, dst = zface.at[side(off[2])], rzface.at[ZOFF.index(opp)]
-        return pltpu.make_async_remote_copy(
-            src_ref=src, dst_ref=dst, send_sem=send_sem.at[n], recv_sem=recv_sem.at[slot],
-            device_id={a: i + o for a, i, o in zip(AXES, here, off)}, device_id_type=MESH,
-        )
+        send_faces(c)
 
     for off in OFFS:
         @pl.when(there(off))
@@ -317,18 +356,16 @@
     for off in OFFS:
         @pl.when(there(off))
         def _(off=off):
-            n = OFFS.index(off)
-            if off[0]:
-                dst = rpack.at[XOFF.index(off)]
-            elif off[1] and off[2]:
-                dst = ryz.at[YZOFF.index(off)]
-            elif off[1]:
-                dst = ryface.at[YOFF.index(off)]
-            else:
-                dst = rzface.at[ZOFF.index(off)]
-            pltpu.make_async_copy(dst, dst, recv_sem.at[n]).wait()
-
-    total_rows = planes * rows
+            dst = landing(off)
+            pltpu.make_async_copy(dst, dst, recv_sem.at[OFFS.index(off)]).wait()
+
+    for k, off in enumerate(FACES):
+        @pl.when(there(off))
+        def _(k=k, off=off):
+            for c in range(4):
+                dst = (ryface if off[1] else rzface).at[k % 2, c]
+                pltpu.make_async_copy(dst, dst, frecv.at[k, c]).wait()
+
     pshape = (4, total_rows)
     place = lax.broadcasted_iota(jnp.int32, (1, total_rows), 1)
     for s, dx in ((0, 1), (1, -1)):
@@ -390,9 +427,14 @@
         def _(off=off):
             copy_to(off).wait_send()
 
-    @pl.loop(1, count)
-    def _(step):
-        scalar_copy(step).wait_send()
+    for off in FACES:
+        @pl.when(there(off))
+        def _(off=off):
+            for c in range(4):
+                face_copy(off, c).wait_send()
+
+    sent = parts.at[pl.ds(0, count - 1)]
+    pltpu.make_async_copy(sent, sent, ssend).wait()
 
 
 def finish(a_ref, b_ref, s_ref, r_hbm, k_hbm, e_hbm, r, k, e, sem):
@@ -456,6 +498,8 @@
             pltpu.SemaphoreType.DMA((len(OFFS),)),
             pltpu.SemaphoreType.DMA,
             pltpu.SemaphoreType.DMA,
+            pltpu.SemaphoreType.DMA((len(FACES), 4)),
+            pltpu.SemaphoreType.DMA((len(FACES), 4)),
         ],
         compiler_params=pltpu.CompilerParams(
             collective_id=0, has_side_effects=True, vmem_limit_bytes=32 * 1024 * 1024

time: 16.4 us -> 14.7 us (0.90)
  Pallas kernels: 15.6 us -> 14 us
    pallas_call x1, Pallas kernels: 14.6 us -> 13 us  [per_device(): pl.pallas_call(functools.partial(kernel, sizes), out_shape=(jax.ShapeDtyp...]
where the time goes in v4:
time: 14.7 us; the launch traced here: 14.6 us
  Pallas kernels  14 us (95%)
  between operations  0.64 us (4%)
    pallas_call x1, Pallas kernels, per_device(): pl.pallas_call(functools.partial(kernel, sizes), out_shape=(jax.ShapeDtyp...  13 us
    pallas_call x1, Pallas kernels, per_device(): pl.pallas_call(finish, out_shape=(jax.ShapeDtypeStruct(velocity.shape, f3...  1 us

profile of v4, /device:TPU:0, one launch (start us, length us, event | category | flops | bytes accessed | tf_op | source)
XLA Modules:
  0.0 14.6 jit_solution(17312265406770165355)
XLA Ops:
  0.6 13.0 %shard_map.112 = (f32[3,16,32,128]{3,2,1,0:T(8,128)S(1)}, f32[3,16,32,128]{3,2,1,0:T(8,128)S(1)}, f32[2,128]{1,0:T(2,128)S(1)}) custom-call(f32[3,16,32,128]{3,2,1,0:T(8,128)} %v_hbm.1, bf16[6,16,32,128]{3,2,1,0:T(8,128)(2,1)} %g_hbm.1, bf16[16,32,128]{2,1,0:T(8,128)(2,1)} %m_hbm.1, bf16[256,256]{1,0:T(8,128)(2,1)} %constant.12.clone.dx_hbm, ...), custom_call_target="tpu_custom_call" | custom-call | tf_op jit(solution)/shard_map/pallas_call | solution.py:468
  13.6 1.0 %shard_map.113 = (f32[3,16,32,128]{3,2,1,0:T(8,128)}, f32[1,1]{1,0:T(1,128)}, f32[1,1]{1,0:T(1,128)}) custom-call(f32[3,16,32,128]{3,2,1,0:T(8,128)S(1)} %get-tuple-element.9.a_ref, f32[3,16,32,128]{3,2,1,0:T(8,128)S(1)} %get-tuple-element.10.b_ref, f32[2,128]{1,0:T(2,128)S(1)} %get-tuple-element.11.s_ref), custom_call_target="tpu_custom_call" | custom-call | tf_op jit(solution)/shard_map/pallas_call | solution.py:509
